TPU v7x, 32 devices: a whole 2x2x4 slice. The times are simulated.
32 devices in a mesh: agent: 4 (over x, core), tile: 8 (over z, y).
Axes of the slice: x: 2, y: 2, z: 4, core: 2. Of those that a mesh axis runs over, the one named last changes fastest.
Arguments:
- states: float32 [4, 4, 512, 512], P('agent', None, 'tile'), may hold values from -6 to 6
- sinogram: float32 [256, 4, 128], P('tile'), may hold values from -6 to 6
- blocks: bfloat16 [2048, 128, 128], P('tile'), may hold values from -0.1875 to 0.1875
- block_angle: int32 [2048], P('tile'), may hold values from 0 to 63
- block_detector: int32 [2048], P('tile'), may hold values from 0 to 3
- block_tile: int32 [2048], P('tile'), may hold values from 0 to 255
- conv_first: bfloat16 [3, 3, 3, 32], replicated, may hold values from -3 to 3
- conv_hidden: bfloat16 [3, 2, 3, 3, 32, 32], replicated, may hold values from -0.5 to 0.5
- conv_last: bfloat16 [3, 3, 3, 32], replicated, may hold values from -0.375 to 0.375
Outputs:
- new_states: float32 [4, 4, 512, 512], P('agent', None, 'tile')
Inputs may be any that keep to these rules, and one draw needn't show every extreme that they name: `block_angle`: each block's angle index. `block_detector`: each block's detector block. `block_tile`: tile index among the 256 pixel tiles of the block's device.
All inputs are finite; a program needn't handle non-finite values.
Results may differ from a plain program's by a relative error of at most 0.0051.
Values may be sent and summed in bfloat16 or wider, within the bound.
A program may use at most 256 MiB of HBM per device.

v0:
```python
import functools

import jax
import jax.numpy as jnp
import numpy as np
from jax import lax
from jax.experimental import pallas as pl
from jax.experimental.pallas import tpu as pltpu
from jax.sharding import PartitionSpec as P

DATA_STEPS = 2
MESH = pl.DeviceIdType.MESH
LANES = 128
GROUPS = 16
STRIPS = 16


def extended(cells, axis, dim, width):
    count = lax.axis_size(axis)
    ends = count - 1
    head = lax.slice_in_dim(cells, 0, width, axis=dim)
    tail = lax.slice_in_dim(cells, cells.shape[dim] - width, cells.shape[dim], axis=dim)
    return jnp.concatenate(
        [
            lax.ppermute(tail, axis, [(i, (i + 1) % count) for i in range(ends)]),
            cells,
            lax.ppermute(head, axis, [((i + 1) % count, i) for i in range(ends)]),
        ],
        axis=dim,
    )


def band(weight, rows_in, first_row):
    taps_row = np.zeros((3, rows_in, 4), np.float32)
    for row_in in range(rows_in):
        for row in range(4):
            tap = row_in + first_row - row + 1
            if 0 <= tap < 3:
                taps_row[tap, row_in, row] = 1
    return spread(weight, taps_row)


def band_same(weight):
    parts = []
    for tap in range(3):
        taps_row = np.zeros((3, 4, 4), np.float32)
        taps_row[tap] = np.eye(4)
        parts.append(spread(weight, taps_row))
    return jnp.stack(parts)


def spread(weight, taps_row):
    taps_position = np.zeros((3, 4, 2), np.float32)
    for k in range(4):
        for par in range(2):
            if 0 <= k - par < 3:
                taps_position[k - par, k, par] = 1
    half = jnp.einsum("irs,ijcd->jrscd", jnp.asarray(taps_row, jnp.bfloat16), weight, preferred_element_type=jnp.float32)
    full = jnp.einsum(
        "jkp,jrscd->krcpsd", jnp.asarray(taps_position, jnp.bfloat16), half.astype(jnp.bfloat16), preferred_element_type=jnp.float32
    )
    return full.astype(jnp.bfloat16)


def hidden_band(weight):
    layers, _, _, inner, _ = weight.shape
    padded = jnp.pad(jnp.swapaxes(weight, 1, 2), ((0, 0), (1, 1), (2, 2), (0, 0), (0, 0)))
    parts = [padded[:, 1 - par : 5 - par, 3 - row : 7 - row] for par in range(2) for row in range(4)]
    return jnp.concatenate(parts, axis=-1).reshape(layers, 16 * inner, 8 * inner)


def hidden_same(weight):
    layers, _, _, inner, _ = weight.shape
    padded = jnp.pad(weight, ((0, 0), (0, 0), (1, 1), (0, 0), (0, 0)))
    wide = jnp.concatenate([padded[:, :, 1 - par : 5 - par] for par in range(2) for _ in range(4)], axis=-1)
    lane_row = (np.arange(8 * inner) // inner) % 4
    mask = jnp.asarray(lane_row[None, :] == np.arange(4)[:, None])
    full = jnp.where(mask[:, None, :], wide[:, :, :, None], jnp.zeros((), wide.dtype))
    return full.reshape(layers, 48 * inner, 8 * inner)


def net_weights(first, hidden, last, axial):
    inner = hidden.shape[-1]
    depth = 16 * inner
    if axial:
        w_first = band_same(first[:, :, None, :]).reshape(48, 8 * inner)
    else:
        w_first = band(first[:, :, None, :], 4, 0).reshape(16, 8 * inner)

    def last_part(weight):
        if axial:
            return band_same(weight).reshape(3 * depth, 8)
        return band(weight, 4, 0).reshape(depth, 8)

    w_hidden = hidden_same(hidden) if axial else hidden_band(hidden)
    w_last = jnp.tile(last_part(last[:, :, :, None]), (1, GROUPS))
    return w_first, w_hidden, w_last


def net_kernel(plan, x_ref, w1_ref, wh_ref, wl_ref, out_ref, even, odd):
    group, size, layers, masked, first_out, out_chunks = plan
    chunks = x_ref.shape[0]
    pairs = chunks * group
    step_rows = group * size

    if masked:
        place = lax.axis_index("tile")
        at_start = place == 0
        at_end = place == lax.axis_size("tile") - 1

    for side in range(2):
        for ref in (even, odd):
            ref[side, 0] = jnp.zeros(ref.shape[2:], ref.dtype)
            ref[side, pairs + 1] = jnp.zeros(ref.shape[2:], ref.dtype)

    def store(side, c, y):
        y = jnp.maximum(y, 0.0)
        if masked:
            outside = (at_start & (c < first_out)) | (at_end & (c >= chunks - first_out))
            y = y * jnp.where(outside, 0.0, 1.0)
        y = y.astype(jnp.bfloat16)
        even[side, pl.ds(1 + c * group, group)] = y[:, :LANES].reshape(group, size, LANES)
        odd[side, pl.ds(1 + c * group, group)] = y[:, LANES:].reshape(group, size, LANES)

    def gathered(side, c):
        low = c * group
        sources = ((odd, low), (even, low + 1), (odd, low + 1), (even, low + 2))
        parts = [ref[side, pl.ds(at, group)].reshape(step_rows, LANES) for ref, at in sources]
        return jnp.concatenate(parts, axis=1)

    def first_step(c, carry):
        y = lax.dot_general(
            x_ref[c], w1_ref[...], (((0,), (0,)), ((), ())), preferred_element_type=jnp.float32
        )
        store(0, c, y)
        return carry

    lax.fori_loop(0, chunks, first_step, 0)
    for layer in range(layers):
        source, target = layer % 2, (layer + 1) % 2

        def hidden_step(c, carry):
            y = jnp.dot(gathered(source, c), wh_ref[layer], preferred_element_type=jnp.float32)
            store(target, c, y)
            return carry

        lax.fori_loop(0, chunks, hidden_step, 0)

    lane_group = lax.broadcasted_iota(jnp.int32, (step_rows, LANES), 1) // 8

    def last_step(c, carry):
        y = jnp.dot(gathered(layers % 2, c + first_out), wl_ref[...], preferred_element_type=jnp.float32)
        out_ref[c // GROUPS] = jnp.where(lane_group == c % GROUPS, y, out_ref[c // GROUPS])
        return carry

    out_ref[...] = jnp.zeros_like(out_ref)
    lax.fori_loop(0, out_chunks, last_step, 0)


def run_net(x, weights, group, size, masked, first_out, out_chunks):
    w_first, w_hidden, w_last = weights
    chunks = x.shape[0]
    pairs = chunks * group
    layers = w_hidden.shape[0]
    out_blocks = -(-out_chunks // GROUPS)
    plan = (group, size, layers, masked, first_out, out_chunks)
    whole = pl.BlockSpec(memory_space=pltpu.VMEM)
    cells = pairs * size * 2 * LANES
    return pl.pallas_call(
        functools.partial(net_kernel, plan),
        out_shape=jax.ShapeDtypeStruct((out_blocks, group * size, LANES), jnp.float32),
        in_specs=[whole] * 4,
        out_specs=whole,
        scratch_shapes=[
            pltpu.VMEM((2, pairs + 2, size, LANES), jnp.bfloat16),
            pltpu.VMEM((2, pairs + 2, size, LANES), jnp.bfloat16),
        ],
        cost_estimate=pl.CostEstimate(flops=cells * 512 * 2 * 3, bytes_accessed=x.size * 2, transcendentals=0),
        compiler_params=pltpu.CompilerParams(vmem_limit_bytes=60 * 1024 * 1024),
        name="net_masked" if masked else "net_plain",
    )(x, w_first, w_hidden, w_last)


def axial_kernel(plan, x_ref, w1_ref, wh_ref, wl_ref, out_ref, even, odd):
    group, layers, halo = plan
    rows, _, cells = x_ref.shape
    pairs = cells // STRIPS
    step_rows = group * cells
    place = lax.axis_index("tile")
    at_start = place == 0
    at_end = place == lax.axis_size("tile") - 1
    strip = lax.broadcasted_iota(jnp.int32, (STRIPS, LANES), 0)

    for side in range(2):
        for ref in (even, odd):
            ref[side, 0] = jnp.zeros(ref.shape[2:], ref.dtype)
            ref[side, rows + 1] = jnp.zeros(ref.shape[2:], ref.dtype)

    def store(side, row, count, y):
        outside = (at_start & (row < halo)) | (at_end & (row >= rows - halo))
        y = jnp.maximum(y, 0.0) * jnp.where(outside, 0.0, 1.0)
        y = y.reshape(count, pairs, STRIPS, 2 * LANES)
        at = pl.ds(row + 1, count)
        even[side, at, pl.ds(1, pairs)] = y[..., :LANES].astype(jnp.bfloat16)
        odd[side, at, pl.ds(1, pairs)] = y[..., LANES:].astype(jnp.bfloat16)
        for r in range(count):
            before = y[r, pairs - 1, :, LANES:]
            before = jnp.where(strip == 0, 0.0, pltpu.roll(before, 1, 0))
            odd[side, row + 1 + r, 0] = before.astype(jnp.bfloat16)
            after = y[r, 0, :, :LANES]
            after = jnp.where(strip == STRIPS - 1, 0.0, pltpu.roll(after, STRIPS - 1, 0))
            even[side, row + 1 + r, pairs + 1] = after.astype(jnp.bfloat16)

    def gathered(side, row):
        parts = []
        for tap in range(3):
            at = pl.ds(row + tap, group)
            for ref, first in ((odd, 0), (even, 1), (odd, 1), (even, 2)):
                parts.append(ref[side, at, pl.ds(first, pairs)].reshape(step_rows, LANES))
        return jnp.concatenate(parts, axis=1)

    def first_step(row, carry):
        y = lax.dot_general(
            x_ref[row], w1_ref[...], (((0,), (0,)), ((), ())), preferred_element_type=jnp.float32
        )
        store(0, row, 1, y)
        return carry

    lax.fori_loop(0, rows, first_step, 0, unroll=4)
    for layer in range(layers):
        source, target = layer % 2, (layer + 1) % 2

        def hidden_step(c, carry):
            y = jnp.dot(gathered(source, c * group), wh_ref[layer], preferred_element_type=jnp.float32)
            store(target, c * group, group, y)
            return carry

        lax.fori_loop(0, rows // group, hidden_step, 0)

    lane_group = lax.broadcasted_iota(jnp.int32, (step_rows, LANES), 1) // 8

    def last_step(c, carry):
        y = jnp.dot(gathered(layers % 2, halo + c * group), wl_ref[...], preferred_element_type=jnp.float32)
        out_ref[c // GROUPS] = jnp.where(lane_group == c % GROUPS, y, out_ref[c // GROUPS])
        return carry

    out_ref[...] = jnp.zeros_like(out_ref)
    lax.fori_loop(0, (rows - 2 * halo) // group, last_step, 0)


def axial_net(rimmed, weights, halo):
    slices, rows, columns = rimmed.shape
    group = 4
    local = rows - 2 * halo
    pairs = columns // (2 * STRIPS)
    cells = pairs * STRIPS
    column = jnp.arange(columns, dtype=jnp.int32)[:, None, None, None]
    k = jnp.arange(4, dtype=jnp.int32)[None, :, None, None]
    i = jnp.arange(pairs, dtype=jnp.int32)[None, None, :, None]
    j = jnp.arange(STRIPS, dtype=jnp.int32)[None, None, None, :]
    place = (column == j * (2 * pairs) + 2 * i + k - 1).astype(jnp.bfloat16).reshape(columns, 4, cells)
    padded = jnp.pad(rimmed, ((0, 0), (1, 1), (0, 0)))
    x = jnp.einsum("zrc,ckm->kzrm", padded, place, preferred_element_type=jnp.float32).astype(jnp.bfloat16)
    x = jnp.stack([x[:, :, tap : tap + rows] for tap in range(3)])
    x = jnp.transpose(x, (3, 0, 1, 2, 4)).reshape(rows, 12 * slices, cells)
    layers = weights[1].shape[0]
    whole = pl.BlockSpec(memory_space=pltpu.VMEM)
    out_chunks = local // group
    out = pl.pallas_call(
        functools.partial(axial_kernel, (group, layers, halo)),
        out_shape=jax.ShapeDtypeStruct((-(-out_chunks // GROUPS), group * cells, LANES), jnp.float32),
        in_specs=[whole] * 4,
        out_specs=whole,
        scratch_shapes=[
            pltpu.VMEM((2, rows + 2, pairs + 2, STRIPS, LANES), jnp.bfloat16),
            pltpu.VMEM((2, rows + 2, pairs + 2, STRIPS, LANES), jnp.bfloat16),
        ],
        compiler_params=pltpu.CompilerParams(vmem_limit_bytes=60 * 1024 * 1024),
        name="net_axial",
    )(x, *weights)
    out = out.astype(jnp.bfloat16).reshape(out.shape[0], group, cells, LANES)
    out = jnp.swapaxes(out, 2, 3).reshape(out.shape[0], group, GROUPS, 2, slices, cells)
    net = jnp.einsum("bgqpzm,cpm->zbqgc", out, place[:, 1:3], preferred_element_type=jnp.float32)
    return net.reshape(slices, -1, columns)[:, :local]


def sagittal_net(rimmed, weights, halo):
    slices, rows, columns = rimmed.shape
    padded = jnp.pad(rimmed, ((0, 0), (1, 1), (0, 0)))
    x = jnp.stack([padded[:, k : k + rows : 2] for k in range(4)], axis=0)
    x = jnp.transpose(x, (2, 0, 1, 3)).reshape(rows // 2, 4 * slices, columns)
    local = rows - 2 * halo
    out = run_net(x, weights, 1, columns, True, halo // 2, local // 2)
    out = out.reshape(out.shape[0], columns, GROUPS, 2, slices)
    return jnp.transpose(out, (4, 0, 2, 3, 1)).reshape(slices, -1, columns)[:, :local]


def coronal_net(rounded, weights):
    slices, rows, columns = rounded.shape
    group = 512 // rows
    chunks = columns // (2 * group)
    turned = jnp.transpose(jnp.pad(rounded, ((0, 0), (0, 0), (1, 1))), (2, 0, 1))
    x = jnp.stack([turned[k : k + columns : 2] for k in range(4)], axis=1)
    x = x.reshape(chunks, group, 4 * slices, rows)
    x = jnp.transpose(x, (0, 2, 1, 3)).reshape(chunks, 4 * slices, group * rows)
    out = run_net(x, weights, group, rows, False, 0, chunks)
    out = out.reshape(out.shape[0], group, rows, GROUPS, 2, slices)
    return jnp.transpose(out, (5, 2, 0, 3, 1, 4)).reshape(slices, rows, -1)[:, :, :columns]


def ray_kernel(count, part_ref, sino_ref, out_ref, got, fresh, send1, recv1, send2, recv2):
    rows = sino_ref.shape[0]
    agent = lax.axis_index("agent")

    @pl.when(agent == 0)
    def _():
        me = lax.axis_index("tile")
        barrier = pltpu.get_barrier_semaphore()
        for d in range(1, count):
            pl.semaphore_signal(barrier, inc=1, device_id=(agent, lax.rem(me + d, count)), device_id_type=MESH)
        pl.semaphore_wait(barrier, count - 1)

        def part_copy(d):
            peer = lax.rem(me + d, count)
            return pltpu.make_async_remote_copy(
                src_ref=part_ref.at[peer],
                dst_ref=got.at[d],
                send_sem=send1.at[d],
                recv_sem=recv1.at[d],
                device_id=(agent, peer),
                device_id_type=MESH,
            )

        for d in range(1, count):
            part_copy(d).start()
        total = part_ref[me].astype(jnp.float32) - sino_ref[...]
        for d in range(1, count):
            part_copy(d).wait_recv()
            total = total + got[d].astype(jnp.float32)
        fresh[...] = total.astype(jnp.bfloat16)

        def rest_copy(d):
            return pltpu.make_async_remote_copy(
                src_ref=fresh,
                dst_ref=got2_slot(me),
                send_sem=send2.at[d],
                recv_sem=recv2.at[d],
                device_id=(agent, lax.rem(me + d, count)),
                device_id_type=MESH,
            )

        def got2_slot(slot):
            return out_ref.at[slot]

        for d in range(1, count):
            rest_copy(d).start()
        out_ref[me] = fresh[...]
        for d in range(1, count):
            rest_copy(d).wait_recv()
        for d in range(1, count):
            part_copy(d).wait_send()
            rest_copy(d).wait_send()

    @pl.when(agent != 0)
    def _():
        out_ref[...] = jnp.zeros_like(out_ref)


def ray_exchange(part, sinogram, count):
    rows = sinogram.shape[0]
    whole = pl.BlockSpec(memory_space=pltpu.VMEM)
    return pl.pallas_call(
        functools.partial(ray_kernel, count),
        out_shape=jax.ShapeDtypeStruct((count, rows, LANES), jnp.bfloat16),
        in_specs=[whole] * 2,
        out_specs=whole,
        scratch_shapes=[
            pltpu.VMEM((count, rows, LANES), jnp.bfloat16),
            pltpu.VMEM((rows, LANES), jnp.bfloat16),
            pltpu.SemaphoreType.DMA((count,)),
            pltpu.SemaphoreType.DMA((count,)),
            pltpu.SemaphoreType.DMA((count,)),
            pltpu.SemaphoreType.DMA((count,)),
        ],
        compiler_params=pltpu.CompilerParams(collective_id=0, has_side_effects=True),
        name="ray_exchange",
    )(part, sinogram)


def agent_kernel(own_ref, out_ref, near, pair, far, send, recv):
    me = lax.axis_index("agent")
    tile = lax.axis_index("tile")
    partner = me + 1 - 2 * (me % 2)
    across = (me + 2) % 4
    barrier = pltpu.get_barrier_semaphore()
    for peer in (partner, across):
        pl.semaphore_signal(barrier, inc=1, device_id=(peer, tile), device_id_type=MESH)
    pl.semaphore_wait(barrier, 2)

    first = pltpu.make_async_remote_copy(
        src_ref=own_ref,
        dst_ref=near,
        send_sem=send.at[0],
        recv_sem=recv.at[0],
        device_id=(partner, tile),
        device_id_type=MESH,
    )
    first.start()
    first.wait()
    pair[...] = (own_ref[...].astype(jnp.float32) + near[...].astype(jnp.float32)).astype(jnp.bfloat16)
    second = pltpu.make_async_remote_copy(
        src_ref=pair,
        dst_ref=far,
        send_sem=send.at[1],
        recv_sem=recv.at[1],
        device_id=(across, tile),
        device_id_type=MESH,
    )
    second.start()
    second.wait()
    out_ref[...] = near[...].astype(jnp.float32) + far[...].astype(jnp.float32)


def agent_sum(own):
    whole = pl.BlockSpec(memory_space=pltpu.VMEM)
    return pl.pallas_call(
        agent_kernel,
        out_shape=jax.ShapeDtypeStruct(own.shape, jnp.float32),
        in_specs=[whole],
        out_specs=whole,
        scratch_shapes=[
            pltpu.VMEM(own.shape, jnp.bfloat16),
            pltpu.VMEM(own.shape, jnp.bfloat16),
            pltpu.VMEM(own.shape, jnp.bfloat16),
            pltpu.SemaphoreType.DMA((2,)),
            pltpu.SemaphoreType.DMA((2,)),
        ],
        compiler_params=pltpu.CompilerParams(collective_id=1, has_side_effects=True),
        name="agent_sum",
    )(own)


def per_device(
    states,
    sinogram,
    blocks,
    block_angle,
    block_detector,
    block_tile,
    conv_first,
    conv_hidden,
    conv_last,
):
    current = states[0]
    slices, local_rows, image_columns = current.shape
    tile_count = lax.axis_size("tile")
    agent_place = lax.axis_index("agent")
    is_data = agent_place == 0
    tiles_here = local_rows * image_columns // LANES
    rays_here = sinogram.shape[0]
    ray_total = rays_here * tile_count
    part_shape = (tile_count, rays_here * slices, LANES)

    def ray_hot():
        ray_index = block_angle * (image_columns // LANES) + block_detector
        return ray_index[:, None] == jnp.arange(ray_total, dtype=jnp.int32)[None, :]

    def tile_hot():
        return block_tile[:, None] == jnp.arange(tiles_here, dtype=jnp.int32)[None, :]

    def project(volume):
        pixels = volume.astype(jnp.bfloat16).reshape(slices, tiles_here, LANES)
        picked = jnp.einsum(
            "bt,ztp->bzp", tile_hot().astype(jnp.bfloat16), pixels, preferred_element_type=jnp.float32
        ).astype(jnp.bfloat16)
        projected = jnp.einsum("bzp,bqp->bzq", picked, blocks, preferred_element_type=jnp.float32)
        partial_value = jnp.einsum(
            "br,bzq->rzq",
            ray_hot().astype(jnp.float32),
            projected,
            precision=lax.Precision.HIGHEST,
        )
        return partial_value.astype(jnp.bfloat16).reshape(part_shape)

    def spread_back(residual):
        residual = residual.reshape(ray_total, slices, LANES)
        picked = jnp.einsum(
            "br,rzq->bzq", ray_hot().astype(jnp.bfloat16), residual, preferred_element_type=jnp.float32
        ).astype(jnp.bfloat16)
        contribution = jnp.einsum("bzq,bqp->bzp", picked, blocks, preferred_element_type=jnp.float32)
        summed = jnp.einsum(
            "bt,bzp->ztp",
            tile_hot().astype(jnp.float32),
            contribution,
            precision=lax.Precision.HIGHEST,
        )
        return summed.reshape(slices, local_rows, image_columns)

    halo = conv_hidden.shape[1] + 2
    rounded = current.astype(jnp.bfloat16)
    rimmed = extended(rounded, "tile", 1, halo)
    no_part = jnp.zeros(part_shape, jnp.bfloat16)

    def reflect_of(net):
        return 2.0 * (current - net) - current

    def weights_of(o):
        return net_weights(conv_first[o], conv_hidden[o], conv_last[o], o == 0)

    def data_start():
        return project(current), current

    def axial_only():
        return no_part, reflect_of(axial_net(rimmed, weights_of(0), halo))

    def sagittal_only():
        return no_part, reflect_of(sagittal_net(rimmed, weights_of(1), halo))

    def coronal_only():
        return no_part, reflect_of(coronal_net(rounded, weights_of(2)))

    part, held = lax.switch(agent_place, [data_start, axial_only, sagittal_only, coronal_only])
    own_sinogram = sinogram.reshape(rays_here * slices, LANES)

    for step in range(DATA_STEPS):
        residual = ray_exchange(part, own_sinogram, tile_count)
        if step < DATA_STEPS - 1:

            def advance(held, residual):
                moved = held - 0.8 * spread_back(residual)
                return project(moved), moved

            part, held = lax.cond(is_data, advance, lambda h, r: (no_part, h), held, residual)
        else:

            def settle(held, residual):
                moved = held - 0.8 * spread_back(residual)
                return 2.0 * moved - current

            reflect = lax.cond(is_data, settle, lambda h, r: h, held, residual)

    sent = reflect.astype(jnp.bfloat16).reshape(slices * local_rows, image_columns)
    others = agent_sum(sent).reshape(reflect.shape)
    new_states = 0.5 * current + 0.25 * others - 0.25 * reflect
    return new_states[None]


def solution(mesh):
    placed = (
        P("agent", None, "tile", None),
        P("tile", None, None),
        P("tile", None, None),
        P("tile"),
        P("tile"),
        P("tile"),
        P(),
        P(),
        P(),
    )
    return jax.shard_map(
        per_device,
        mesh=mesh,
        in_specs=placed,
        out_specs=P("agent", None, "tile", None),
        check_vma=False,
    )
```

profile of v0, /device:TPU:0, one launch (start us, length us, event | category | flops | bytes accessed | tf_op | source)
XLA Modules:
  0.0 101.7 jit_solution(17438033776436263919)
XLA Ops:
  0.0 1.1 %bitcast_convert_fusion = bf16[4,64,512]{2,1,0:T(8,128)(2,1)S(1)} fusion(f32[1,4,64,512]{3,2,1,0:T(8,128)} %param.38), kind=kLoop, calls=%fused_computation.182 | loop fusion | flops 131072 | bytes 786432 | tf_op jit(solution)/shard_map/convert_element_type | solution.py:500
  1.1 4.9 %collective-permute-start = (bf16[4,4,512]{2,1,0:T(4,128)(2,1)S(1)}, bf16[4,4,512]{2,1,0:T(4,128)(2,1)S(1)}, u32[]{:S(2)}, u32[]{:S(2)}) collective-permute-start(bf16[4,4,512]{2,1,0:T(4,128)(2,1)S(1)} %get-tuple-element.355), channel_id=1, source_target_pairs={{0,1},{1,2},{2,3},{3,4},{4,5},{5,6},{6,7},{8,9},{9,10},{10,11},{11... | collective-permute-start | bytes 49160 | tf_op jit(solution)/shard_map/ppermute | solution.py:25
  6.0 1.3 %collective-permute-start.1 = (bf16[4,4,512]{2,1,0:T(4,128)(2,1)S(1)}, bf16[4,4,512]{2,1,0:T(4,128)(2,1)S(1)}, u32[]{:S(2)}, u32[]{:S(2)}) collective-permute-start(bf16[4,4,512]{2,1,0:T(4,128)(2,1)S(1)} %get-tuple-element.356), channel_id=1, source_target_pairs={{1,0},{2,1},{3,2},{4,3},{5,4},{6,5},{7,6},{9,8},{10,9},{11,10},{12... | collective-permute-start | bytes 49160 | tf_op jit(solution)/shard_map/ppermute | solution.py:27
  7.4 4.2 %collective-permute-done.1 = bf16[4,4,512]{2,1,0:T(4,128)(2,1)S(1)} collective-permute-done((bf16[4,4,512]{2,1,0:T(4,128)(2,1)S(1)}, bf16[4,4,512]{2,1,0:T(4,128)(2,1)S(1)}, u32[]{:S(2)}, u32[]{:S(2)}) %collective-permute-start.1) | collective-permute-done | bytes 16416 | tf_op jit(solution)/shard_map/ppermute | solution.py:27
  11.7 11.7 %conditional.3 = (bf16[8,128,128]{2,1,0:T(8,128)(2,1)S(1)}, f32[4,64,512]{2,0,1:T(4,128)}, f32[4,64,512]{2,1,0:T(8,128)S(1)}) conditional(s32[]{:T(128)} %clamp.3, (s32[256]{0:T(256)}, s32[256]{0:T(256)}, s32[256]{0:T(256)}, f32[4,64,512]{2,1,0:T(8,128)}, bf16[256,128,128]{2,1,0:T(8,128)(2,1)}) %tuple.107, ...), branch_computations={%region_0.0_spmd, %region_1.2_spmd.clone, %region_2.3_spmd, %regio... | conditional | flops 14496871424 | bytes 25851226 | solution.py:522
  11.8 2.2 %fusion.98 = (bf16[4,64,512]{2,0,1:T(4,128)(2,1)S(1)}, f32[4,64,512]{2,0,1:T(4,128)}) fusion(f32[4,64,512]{2,1,0:T(8,128)} %get-tuple-element.359), kind=kLoop, calls=%fused_computation.183 | loop fusion | flops 131072 | bytes 1310720 | tf_op jit(solution)/shard_map/cond/branch_0_fun/convert_element_type | solution.py:472
  14.6 7.8 %fusion.1 = f32[256,4,128]{2,1,0:T(4,128)S(1)} fusion(bf16[256,128,128]{2,1,0:T(8,128)(2,1)} %get-tuple-element.122, bf16[256,4,128]{2,0,1:T(8,128)(2,1)S(1)} %convolution_convert_fusion.1), kind=kOutput, calls=%fused_computation.3 | convolution fusion | flops 33554432 | bytes 9175040 | tf_op jit(solution)/shard_map/cond/branch_0_fun/bzp,bqp->bzq/dot_general | solution.py:476
  23.4 15.9 %ray_exchange.2 = bf16[8,128,128]{2,1,0:T(8,128)(2,1)S(1)} custom-call(bf16[8,128,128]{2,1,0:T(8,128)(2,1)S(1)} %get-tuple-element.177.part_ref, f32[128,128]{1,0:T(8,128)} %bitcast.437), custom_call_target="tpu_custom_call" | custom-call | tf_op jit(solution)/shard_map/ray_exchange/pallas_call | solution.py:372
  39.3 17.9 %conditional.4 = (bf16[8,128,128]{2,1,0:T(8,128)(2,1)S(1)}, f32[4,64,512]{2,1,0:T(8,128)S(1)}) conditional(s32[]{:T(128)} %convert_element_type.242, f32[4,64,512]{2,1,0:T(8,128)S(1)} %get-tuple-element.323, (s32[256]{0:T(256)}, s32[256]{0:T(256)}, s32[256]{0:T(256)}, bf16[8,128,128]{2,1,0:T(8,128)(2,1)S(1)}, bf16[256,128,128]{2,1,0:T(8,128)(2,1)}, ...), branch_computations={%region_4.5_spmd, %region_5.6_spmd} | conditional | flops 1007682048 | bytes 26225708 | solution.py:533
  39.3 0.8 multiply_add_fusion.1
  40.4 5.7 %fusion.36 = f32[256,4,128]{2,1,0:T(4,128)S(1)} fusion(bf16[256,128,128]{2,1,0:T(8,128)(2,1)} %get-tuple-element.164, bf16[256,4,128]{2,0,1:T(8,128)(2,1)S(1)} %convolution_convert_fusion.12), kind=kOutput, calls=%fused_computation.85 | convolution fusion | flops 33554432 | bytes 9175040 | tf_op jit(solution)/shard_map/cond/branch_1_fun/bzq,bqp->bzp/dot_general | solution.py:490
  46.1 0.7 fusion.31
  47.0 1.2 %fusion.99 = (bf16[4,64,512]{2,1,0:T(8,128)(2,1)S(1)}, f32[4,64,512]{2,1,0:T(8,128)S(1)}) fusion(f32[4,64,512]{2,1,0:T(8,128)S(1)} %mul.64, f32[4,64,512]{2,0,1:T(4,128)} %get-tuple-element.322), kind=kLoop, calls=%fused_computation.184 | loop fusion | flops 262144 | bytes 1835008 | tf_op jit(solution)/shard_map/cond/branch_1_fun/convert_element_type | solution.py:472
  48.7 7.8 %fusion.34 = f32[256,4,128]{2,1,0:T(4,128)S(1)} fusion(bf16[256,128,128]{2,1,0:T(8,128)(2,1)} %get-tuple-element.164, bf16[256,4,128]{2,0,1:T(8,128)(2,1)S(1)} %convolution_convert_fusion.11), kind=kOutput, calls=%fused_computation.83 | convolution fusion | flops 33554432 | bytes 9175040 | tf_op jit(solution)/shard_map/cond/branch_1_fun/bzp,bqp->bzq/dot_general | solution.py:476
  56.5 0.5 convolution_convert_fusion.10
  57.2 14.2 %ray_exchange.3 = bf16[8,128,128]{2,1,0:T(8,128)(2,1)S(1)} custom-call(bf16[8,128,128]{2,1,0:T(8,128)(2,1)S(1)} %get-tuple-element.179.part_ref, f32[128,128]{1,0:T(8,128)} %bitcast.438), custom_call_target="tpu_custom_call" | custom-call | tf_op jit(solution)/shard_map/ray_exchange/pallas_call | solution.py:372
  71.5 8.0 %conditional.5 = (f32[4,64,512]{2,1,0:T(8,128)S(1)}) conditional(s32[]{:T(128)} %convert_element_type.242, f32[4,64,512]{2,1,0:T(8,128)S(1)} %get-tuple-element.178, (s32[256]{0:T(256)}, s32[256]{0:T(256)}, bf16[8,128,128]{2,1,0:T(8,128)(2,1)S(1)}, bf16[256,128,128]{2,1,0:T(8,128)(2,1)}, s32[256]{0:T(256)}, /*index=5*/f32[4,64,512]{2,1,0:T(8,128)S(1)}, ...), branch_computations={%region_6.7_spmd, %region_7.8_spmd} | conditional | flops 504103424 | bytes 14951460 | solution.py:540
  71.5 0.7 multiply_add_fusion.2
  72.5 5.7 %fusion.51 = f32[256,4,128]{2,1,0:T(4,128)S(1)} fusion(bf16[256,128,128]{2,1,0:T(8,128)(2,1)} %get-tuple-element.169, bf16[256,4,128]{2,0,1:T(8,128)(2,1)S(1)} %convolution_convert_fusion.13), kind=kOutput, calls=%fused_computation.102 | convolution fusion | flops 33554432 | bytes 9175040 | tf_op jit(solution)/shard_map/cond/branch_1_fun/bzq,bqp->bzp/dot_general | solution.py:490
  78.1 0.7 fusion.49
  79.5 0.7 convert_element_type.244
  80.2 19.4 %agent_sum.1 = f32[256,512]{1,0:T(8,128)} custom-call(bf16[256,512]{1,0:T(8,128)(2,1)} %bitcast.425), custom_call_target="tpu_custom_call" | custom-call | tf_op jit(solution)/shard_map/agent_sum/pallas_call | solution.py:426
  99.7 1.1 %broadcast_multiply_fusion = f32[256,512]{1,0:T(8,128)S(1)} fusion(f32[256,512]{1,0:T(8,128)} %agent_sum.1), kind=kLoop, calls=%fused_computation.181 | loop fusion | flops 131072 | bytes 1048576 | tf_op jit(solution)/shard_map/mul | solution.py:544
  100.7 1.0 subtract_bitcast_fusion
  (34 shorter events, 3.6 us)
Async XLA Ops:
  1.1 6.3 %collective-permute-start = (bf16[4,4,512]{2,1,0:T(4,128)(2,1)S(1)}, bf16[4,4,512]{2,1,0:T(4,128)(2,1)S(1)}, u32[]{:S(2)}, u32[]{:S(2)}) collective-permute-start(bf16[4,4,512]{2,1,0:T(4,128)(2,1)S(1)} %get-tuple-element.355), channel_id=1, source_target_pairs={{0,1},{1,2},{2,3},{3,4},{4,5},{5,6},{6,7},{8,9},{9,10},{10,11},{11... | collective-permute-start | bytes 49160 | tf_op jit(solution)/shard_map/ppermute | solution.py:25
  6.0 5.6 %collective-permute-start.1 = (bf16[4,4,512]{2,1,0:T(4,128)(2,1)S(1)}, bf16[4,4,512]{2,1,0:T(4,128)(2,1)S(1)}, u32[]{:S(2)}, u32[]{:S(2)}) collective-permute-start(bf16[4,4,512]{2,1,0:T(4,128)(2,1)S(1)} %get-tuple-element.356), channel_id=1, source_target_pairs={{1,0},{2,1},{3,2},{4,3},{5,4},{6,5},{7,6},{9,8},{10,9},{11,10},{12... | collective-permute-start | bytes 49160 | tf_op jit(solution)/shard_map/ppermute | solution.py:27
  11.8 2.5 %copy-start.16 = (s32[256]{0:T(256)S(1)}, s32[256]{0:T(256)}, u32[]{:S(2)}) copy-start(s32[256]{0:T(256)} %get-tuple-element.120) | copy-start | bytes 3076 | tf_op jit(solution)/shard_map/cond
  14.5 7.9 %copy-start.22 = (s32[256]{0:T(256)S(1)}, s32[256]{0:T(256)}, u32[]{:S(2)}) copy-start(s32[256]{0:T(256)} %get-tuple-element.118) | copy-start | bytes 3076 | tf_op jit(solution)/shard_map/cond
  14.5 7.9 %copy-start.23 = (s32[256]{0:T(256)S(1)}, s32[256]{0:T(256)}, u32[]{:S(2)}) copy-start(s32[256]{0:T(256)} %get-tuple-element.119) | copy-start | bytes 3076 | tf_op jit(solution)/shard_map/cond
  14.5 8.6 %copy-start.1 = (f32[4,64,512]{2,1,0:T(8,128)S(1)}, f32[4,64,512]{2,1,0:T(8,128)}, u32[]{:S(2)}) copy-start(f32[4,64,512]{2,1,0:T(8,128)} %get-tuple-element.359) | copy-start | bytes 1572868 | tf_op jit(solution)/shard_map/cond
  39.3 32.1 %copy-start = (f32[1,4,64,512]{3,2,1,0:T(8,128)S(1)}, f32[1,4,64,512]{3,2,1,0:T(8,128)}, u32[]{:S(2)}) copy-start(f32[1,4,64,512]{3,2,1,0:T(8,128)} %param.38) | copy-start | bytes 1572868
  40.4 5.7 %copy-start.17 = (s32[256]{0:T(256)S(1)}, s32[256]{0:T(256)}, u32[]{:S(2)}) copy-start(s32[256]{0:T(256)} %get-tuple-element.161) | copy-start | bytes 3076 | tf_op jit(solution)/shard_map/cond
  72.5 5.7 %copy-start.18 = (s32[256]{0:T(256)S(1)}, s32[256]{0:T(256)}, u32[]{:S(2)}) copy-start(s32[256]{0:T(256)} %get-tuple-element.170) | copy-start | bytes 3076 | tf_op jit(solution)/shard_map/cond
where the time goes:
time: 102 us
  Pallas kernels  49.5 us (49%)
  matrix products  30.3 us (30%)
  other arithmetic  9.3 us (9%)
  starting transfers between devices  6.19 us (6%)
  waiting for transfers between devices  4.32 us (4%)
  local copies, waits for them, and re-layouts  1.43 us (1%)
    pallas_call x2, Pallas kernels, ray_exchange(): pl.pallas_call(functools.partial(ray_kernel, count), out_shape=jax.ShapeD...  30.1 us
    pallas_call x1, Pallas kernels, agent_sum(): pl.pallas_call(agent_kernel, out_shape=jax.ShapeDtypeStruct(own.shape, jn...  19.4 us
    dot_general x2, matrix products, project(): jnp.einsum('bzp,bqp->bzq', picked, blocks, preferred_element_type=jnp.flo...  15.6 us
    dot_general x2, matrix products, spread_back(): jnp.einsum('bzq,bqp->bzp', picked, blocks, preferred_element_type=jnp.flo...  11.3 us
    ppermute x1, starting transfers between devices, extended(): lax.ppermute(tail, axis, [(i, (i + 1) % count) for i in range(ends)])  4.9 us
    ppermute x1, waiting for transfers between devices, extended(): lax.ppermute(head, axis, [((i + 1) % count, i) for i in range(ends)])  4.21 us
    convert_element_type x2, other arithmetic, project(): pixels = volume.astype(jnp.bfloat16).reshape(slices, tiles_here, LANES)  3.49 us
  transfers between devices with their start and end apart: 2, of which 2 were waited for; matrix products, arithmetic and copies ran while one was open for 0% of the time, Pallas kernels for 0%

commit v1 on v0

v1 whole, which is shorter than its diff:
```python
import functools

import jax
import jax.numpy as jnp
from jax import lax
from jax.experimental import pallas as pl
from jax.experimental.pallas import tpu as pltpu
from jax.sharding import PartitionSpec as P

DATA_STEPS = 2
MESH = pl.DeviceIdType.MESH
LANES = 128
STRIPS = 16
CHUNK = 32
UNROLL = 8
BF = jnp.bfloat16
F32 = jnp.float32
NATURAL = (0, 1, 2, 3)
EVEN_ORDER = (0, 1, 2, 3)
ODD_ORDER = (1, 0, 3, 2)


def main_cells(offset):
    order = EVEN_ORDER if offset % 2 else ODD_ORDER
    return [(offset, column) for column in order]

def edge_cells(offset):
    return [(offset + 1, 4), (offset, 4), (offset, -1), (offset + 1, -1)]

def window_cells(rows):
    tiles = [main_cells(a) for a in range(rows + 2)]
    return tiles + [edge_cells(a) for a in range(0, rows + 2, 2)]

def spread_lanes(w):
    return jnp.concatenate([w] * (LANES // w.shape[-1]), axis=-1)

def lane_iota(rows):
    return lax.broadcasted_iota(jnp.int32, (rows, LANES), 1)

def slot_mix(rows, taps, column_in, order, width):
    slot = lane_iota(rows) // width
    mixed = jnp.zeros((rows, LANES), F32)
    for place, column in enumerate(order):
        tap = column_in - column + 1
        if 0 <= tap < 3:
            mixed = jnp.where(slot == place, taps[tap], mixed)
    return mixed

def build_first(w_ref, o, w1):
    for k in range(6):
        for half in range(2):
            order = ODD_ORDER if half else EVEN_ORDER
            mixes = []
            for ti in range(3):
                taps = [jnp.broadcast_to(spread_lanes(w_ref[o, ti, tj:tj+1, :].astype(F32)), (16, LANES)) for tj in range(3)]
                mixes.append(slot_mix(16, taps, k - 1, order, 32))
            row = lax.broadcasted_iota(jnp.int32, (16, LANES), 0)
            for t in range(4):
                value = jnp.zeros((16, LANES), F32)
                for ti in range(3):
                    value = jnp.where(row == 2 * t + half + ti, mixes[ti], value)
                at = t * 2 * LANES + half * LANES
                w1[k * 16:(k + 1) * 16, at:at + LANES] = value.astype(BF)

def build_hidden(w_ref, o, layer, wh):
    wide = [[spread_lanes(w_ref[o, layer, ti, tj].astype(F32)) for tj in range(3)] for ti in range(3)]
    inner = wide[0][0].shape[0]
    for n, tile in enumerate(window_cells(2)):
        for slot, (a, column) in enumerate(tile):
            at = n * LANES + slot * inner
            for half in range(2):
                ti = a - (half + 1) + 1
                if 0 <= ti < 3:
                    value = slot_mix(inner, wide[ti], column, ODD_ORDER if half else EVEN_ORDER, inner)
                else:
                    value = jnp.zeros((inner, LANES), F32)
                wh[layer, at:at + inner, half * LANES:(half + 1) * LANES] = value.astype(BF)

def column_of(row):
    inner = row.shape[1]
    r = lax.broadcasted_iota(jnp.int32, (inner, inner), 0)
    c = lax.broadcasted_iota(jnp.int32, (inner, inner), 1)
    picked = jnp.where(r == c, jnp.broadcast_to(row, (inner, inner)), 0.0)
    return jnp.broadcast_to(jnp.sum(picked, axis=1, keepdims=True), (inner, LANES))

def build_last(w_ref, o, wl):
    taps = [[column_of(w_ref[o, ti, tj:tj+1, :].astype(F32)) for tj in range(3)] for ti in range(3)]
    inner = taps[0][0].shape[0]
    lane = lane_iota(inner)
    row8 = lane % 8
    zero = jnp.zeros((inner, LANES), F32)
    rows = []
    for a in range(10):
        line = []
        for tj in range(3):
            value = zero
            for ti in range(3):
                if 0 <= a - ti < 8:
                    value = jnp.where(row8 == a - ti, taps[ti][tj], value)
            line.append(value)
        rows.append(line)
    for n, tile in enumerate(window_cells(8)):
        for slot, (a, column) in enumerate(tile):
            at = n * LANES + slot * inner
            wl[at:at + inner, :] = slot_mix(inner, rows[a], column, EVEN_ORDER, LANES // 4).astype(BF)


def axial_kernel(plan, edges_ref, cur_ref, cf_ref, ch_ref, cl_ref, out_ref, main, edge, w1, wh, wl, raw, xs, place, back, gathered_out):
    halo, chunk = plan
    slices, local, columns = cur_ref.shape
    rows = local + 2 * halo
    stored = rows + 8
    groups = columns // 4
    per = groups // STRIPS
    span = slices * groups
    layers = ch_ref.shape[1]
    tile = lax.axis_index("tile")
    at_start = tile == 0
    at_end = tile == lax.axis_size("tile") - 1
    fill_rows(raw, edges_ref, cur_ref, stored, halo)

    build_first(cf_ref, 0, w1)
    for layer in range(layers):
        build_hidden(ch_ref, 0, layer, wh)
    build_last(cl_ref, 0, wl)

    col = lax.broadcasted_iota(jnp.int32, (columns, groups), 0)
    m = lax.broadcasted_iota(jnp.int32, (columns, groups), 1)
    first_col = 4 * ((m % STRIPS) * per + m // STRIPS)
    for k in range(6):
        place[:, k * groups:(k + 1) * groups] = jnp.where(col == first_col + (k - 1), 1.0, 0.0).astype(BF)
    m = lax.broadcasted_iota(jnp.int32, (groups, columns), 0)
    col = lax.broadcasted_iota(jnp.int32, (groups, columns), 1)
    first_col = 4 * ((m % STRIPS) * per + m // STRIPS)
    for k in range(4):
        back[k * groups:(k + 1) * groups, :] = jnp.where(col == first_col + k, 1.0, 0.0).astype(BF)
    xs[...] = jnp.dot(raw[...].astype(BF), place[...], preferred_element_type=F32)

    slot = lane_iota(STRIPS) // (LANES // 4)
    even_slots = (slot == 0) | (slot == 3)
    right_slots = slot < 2
    strip = lax.broadcasted_iota(jnp.int32, (STRIPS, LANES), 0)
    zero_tile = jnp.zeros((slices, per, STRIPS, LANES), BF)

    for side in range(2):
        for r in (0, 1, 2, rows - 1, rows, rows + 1):
            main[side, r] = zero_tile
        for e in (0, 1, rows // 2 - 1, rows // 2):
            edge[side, e] = zero_tile

    def put_edge(side, e, odd_row, even_row):
        v = jnp.where(even_slots, even_row, odd_row)
        for z in range(slices):
            for i in range(per):
                if i + 1 < per:
                    right = v[z, i + 1]
                else:
                    right = jnp.where(strip == STRIPS - 1, 0.0, pltpu.roll(v[z, 0], STRIPS - 1, 0))
                if i > 0:
                    left = v[z, i - 1]
                else:
                    left = jnp.where(strip == 0, 0.0, pltpu.roll(v[z, per - 1], 1, 0))
                edge[side, e, z, i] = jnp.where(right_slots, right, left).astype(BF)

    def put_pairs(side, pair, count, y):
        before = main[side, 2 * pair].astype(F32)
        for t in range(count):
            row = 2 * (pair + t)
            outside = (at_start & (row < halo)) | (at_end & (row >= rows - halo))
            v = jnp.maximum(y(t), 0.0) * jnp.where(outside, 0.0, 1.0)
            even_row = v[:, :LANES].reshape(slices, per, STRIPS, LANES)
            odd_row = v[:, LANES:].reshape(slices, per, STRIPS, LANES)
            main[side, row + 1] = even_row.astype(BF)
            main[side, row + 2] = odd_row.astype(BF)
            put_edge(side, pair + t, before, even_row)
            before = odd_row

    def first_step(c, carry):
        parts = []
        for z in range(slices):
            at = pl.ds(pl.multiple_of(z * stored + 8 * c, 8), 16)
            parts.append(jnp.concatenate([xs[at, k * groups:(k + 1) * groups] for k in range(6)], axis=0).astype(BF))
        x = jnp.concatenate(parts, axis=1)
        y = lax.dot_general(x, w1[...], (((0,), (0,)), ((), ())), preferred_element_type=F32)
        put_pairs(0, 4 * c, 4, lambda t: y[:, t * 2 * LANES:(t + 1) * 2 * LANES])
        return carry

    lax.fori_loop(0, rows // 8, first_step, 0)

    def window(side, pair, out_rows):
        parts = [main[side, 2 * pair + a].reshape(span, LANES) for a in range(out_rows + 2)]
        parts += [edge[side, pair + e].reshape(span, LANES) for e in range(out_rows // 2 + 1)]
        return jnp.concatenate(parts, axis=1)

    pairs = rows // 2 - 2
    for layer in range(layers):
        source, target = layer % 2, (layer + 1) % 2

        def hidden_step(c, carry):
            pair = 1 + c * chunk
            x = jnp.concatenate([window(source, pair + t, 2) for t in range(chunk)], axis=0)
            y = jnp.dot(x, wh[layer], preferred_element_type=F32)
            put_pairs(target, pair, chunk, lambda t: y[t * span:(t + 1) * span])
            return carry

        lax.fori_loop(0, pairs // chunk, hidden_step, 0)
        end = rows // 2 - 1
        put_edge(target, end, main[target, 2 * end].astype(F32), jnp.zeros((slices, per, STRIPS, LANES), F32))

    eighths = local // 8
    quad = (lane_iota(span) // 8) % 4

    def last_step(q, carry):
        x = window(layers % 2, halo // 2 + 4 * q, 8)
        y = jnp.dot(x, wl[...], preferred_element_type=F32)
        gathered_out[q // 4] = jnp.where(quad == q % 4, y, gathered_out[q // 4])
        return carry

    gathered_out[...] = jnp.zeros_like(gathered_out)
    lax.fori_loop(0, eighths, last_step, 0)

    for big in range(gathered_out.shape[0]):
        height = min(32, local - 32 * big)
        turned = [gathered_out[big, z * groups:(z + 1) * groups, :].T for z in range(slices)]
        lines = [jnp.concatenate([turned[z][k * 32:(k + 1) * 32] for k in range(4)], axis=1) for z in range(slices)]
        values = jnp.concatenate(lines, axis=0)
        high = values.astype(BF)
        low = (values - high.astype(F32)).astype(BF)
        net = jnp.dot(high, back[...], preferred_element_type=F32) + jnp.dot(low, back[...], preferred_element_type=F32)
        for z in range(slices):
            at = pl.ds(32 * big, height)
            out_ref[z, at, :] = cur_ref[z, at, :] - 2.0 * net[z * 32:z * 32 + height]

def axial_reflect(edges, current, cf, ch, cl, halo):
    slices, local, columns = current.shape
    rows = local + 2 * halo
    groups = columns // 4
    per = groups // STRIPS
    stored = rows + 8
    whole = pl.BlockSpec(memory_space=pltpu.VMEM)
    return pl.pallas_call(
        functools.partial(axial_kernel, (halo, 2)),
        out_shape=jax.ShapeDtypeStruct(current.shape, F32),
        in_specs=[whole] * 5,
        out_specs=whole,
        scratch_shapes=[
            pltpu.VMEM((2, rows + 2, slices, per, STRIPS, LANES), BF),
            pltpu.VMEM((2, rows // 2 + 1, slices, per, STRIPS, LANES), BF),
            pltpu.VMEM((96, 8 * LANES), BF),
            pltpu.VMEM((ch.shape[1], 6 * LANES, 2 * LANES), BF),
            pltpu.VMEM((15 * LANES, LANES), BF),
            pltpu.VMEM((slices * stored, columns), F32),
            pltpu.VMEM((slices * stored, 6 * groups), F32),
            pltpu.VMEM((columns, 6 * groups), BF),
            pltpu.VMEM((4 * groups, columns), BF),
            pltpu.VMEM((-(-local // 32), slices * groups, LANES), F32),
        ],
        compiler_params=pltpu.CompilerParams(vmem_limit_bytes=60 * 1024 * 1024),
        name="net_axial",
    )(edges, current, cf, ch, cl)


def fill_rows(raw, edges_ref, cur_ref, stored, halo):
    slices, local, columns = cur_ref.shape
    zero = jnp.zeros((1, columns), F32)
    tail = jnp.zeros((stored - 1 - local - 2 * halo, columns), F32)
    for z in range(slices):
        above = edges_ref[0, z * halo:(z + 1) * halo, :].astype(F32)
        below = edges_ref[1, z * halo:(z + 1) * halo, :].astype(F32)
        raw[z * stored:(z + 1) * stored, :] = jnp.concatenate([zero, above, cur_ref[z], below, tail], axis=0)


def build_first_plane(w_ref, o, w1):
    row = lax.broadcasted_iota(jnp.int32, (16, LANES), 0)
    for z in range(4):
        mixes = []
        for tj in range(3):
            taps = [jnp.broadcast_to(spread_lanes(w_ref[o, ti, tj:tj+1, :].astype(F32)), (16, LANES)) for ti in range(3)]
            mixes.append(slot_mix(16, taps, z, NATURAL, 32))
        for t in range(8):
            value = jnp.zeros((16, LANES), F32)
            for tj in range(3):
                value = jnp.where(row == t + tj, mixes[tj], value)
            w1[z * 16:(z + 1) * 16, t * LANES:(t + 1) * LANES] = value.astype(BF)

def build_hidden_plane(w_ref, o, layer, wh):
    wide = [[spread_lanes(w_ref[o, layer, ti, tj].astype(F32)) for ti in range(3)] for tj in range(3)]
    inner = wide[0][0].shape[0]
    for a in range(4):
        for z in range(4):
            at = a * LANES + z * inner
            for half in range(2):
                if 0 <= a - half < 3:
                    value = slot_mix(inner, wide[a - half], z, NATURAL, inner)
                else:
                    value = jnp.zeros((inner, LANES), F32)
                wh[layer, at:at + inner, half * LANES:(half + 1) * LANES] = value.astype(BF)

def build_last_plane(w_ref, o, wl):
    taps = [[column_of(w_ref[o, ti, tj:tj+1, :].astype(F32)) for ti in range(3)] for tj in range(3)]
    inner = taps[0][0].shape[0]
    row8 = lane_iota(inner) % 8
    zero = jnp.zeros((inner, LANES), F32)
    for a in range(10):
        line = []
        for ti in range(3):
            value = zero
            for tj in range(3):
                if 0 <= a - tj < 8:
                    value = jnp.where(row8 == a - tj, taps[tj][ti], value)
            line.append(value)
        for z in range(4):
            at = a * LANES + z * inner
            wl[at:at + inner, :] = slot_mix(inner, line, z, NATURAL, LANES // 4).astype(BF)


def plane_kernel(plan, x_ref, cur_ref, cf_ref, ch_ref, cl_ref, out_ref, main, w1, wh, wl, xs, gathered_out):
    o, halo, chunk, strips = plan
    slices, local, span = out_ref.shape
    rows = local + 2 * halo
    stored = rows + 8
    layers = ch_ref.shape[1]
    if halo:
        tile = lax.axis_index("tile")
        at_start = tile == 0
        at_end = tile == lax.axis_size("tile") - 1

    build_first_plane(cf_ref, o, w1)
    for layer in range(layers):
        build_hidden_plane(ch_ref, o, layer, wh)
    build_last_plane(cl_ref, o, wl)
    if halo:
        fill_rows(xs, x_ref, cur_ref, stored, halo)
    else:
        xs[...] = x_ref[...].astype(F32)
    for side in range(2):
        for r in (0, rows + 1):
            main[side, r] = jnp.zeros((span, LANES), BF)

    def put_pairs(side, pair, count, y):
        for t in range(count):
            row = 2 * (pair + t)
            v = jnp.maximum(y(t), 0.0)
            if halo:
                outside = (at_start & (row < halo)) | (at_end & (row >= rows - halo))
                v = v * jnp.where(outside, 0.0, 1.0)
            main[side, row + 1] = v[:, :LANES].astype(BF)
            main[side, row + 2] = v[:, LANES:].astype(BF)

    def ends(side):
        if strips > 1:
            step = span // strips
            main[side, 0, step:span] = main[side, rows, 0:span - step]
            main[side, rows + 1, 0:span - step] = main[side, 1, step:span]

    def first_step(c, carry):
        parts = [xs[pl.ds(pl.multiple_of(z * stored + 8 * c, 8), 16)] for z in range(slices)]
        x = jnp.concatenate(parts, axis=0).astype(BF)
        y = lax.dot_general(x, w1[...], (((0,), (0,)), ((), ())), preferred_element_type=F32)
        put_pairs(0, 4 * c, 4, lambda t: y[:, t * 2 * LANES:(t + 1) * 2 * LANES])
        return carry

    lax.fori_loop(0, rows // 8, first_step, 0)
    ends(0)

    for layer in range(layers):
        source, target = layer % 2, (layer + 1) % 2

        def hidden_step(c, carry):
            pair = c * chunk
            tiles = [main[source, 2 * pair + a] for a in range(2 * chunk + 2)]
            x = jnp.concatenate([jnp.concatenate(tiles[2 * t:2 * t + 4], axis=1) for t in range(chunk)], axis=0)
            y = jnp.dot(x, wh[layer], preferred_element_type=F32)
            put_pairs(target, pair, chunk, lambda t: y[t * span:(t + 1) * span])
            return carry

        lax.fori_loop(0, rows // 2 // chunk, hidden_step, 0)
        ends(target)

    quad = (lane_iota(span) // 8) % 4

    def last_step(q, carry):
        x = jnp.concatenate([main[layers % 2, halo + 8 * q + a] for a in range(10)], axis=1)
        y = jnp.dot(x, wl[...], preferred_element_type=F32)
        gathered_out[q // 4] = jnp.where(quad == q % 4, y, gathered_out[q // 4])
        return carry

    gathered_out[...] = jnp.zeros_like(gathered_out)
    lax.fori_loop(0, local // 8, last_step, 0)
    for big in range(gathered_out.shape[0]):
        height = min(32, local - 32 * big)
        net = gathered_out[big].T
        for z in range(slices):
            at = pl.ds(32 * big, height)
            out_ref[z, at, :] = cur_ref[z, at, :] - 2.0 * net[z * 32:z * 32 + height]

def plane_call(o, x, current, cf, ch, cl, halo, strips):
    slices, local, span = current.shape
    rows = local + 2 * halo
    whole = pl.BlockSpec(memory_space=pltpu.VMEM)
    return pl.pallas_call(
        functools.partial(plane_kernel, (o, halo, 4, strips)),
        out_shape=jax.ShapeDtypeStruct(current.shape, F32),
        in_specs=[whole] * 5, out_specs=whole,
        scratch_shapes=[
            pltpu.VMEM((2, rows + 2, span, LANES), BF),
            pltpu.VMEM((64, 8 * LANES), BF),
            pltpu.VMEM((ch.shape[1], 4 * LANES, 2 * LANES), BF),
            pltpu.VMEM((10 * LANES, LANES), BF),
            pltpu.VMEM((slices * (rows + 8), span), F32),
            pltpu.VMEM((-(-local // 32), span, LANES), F32),
        ],
        compiler_params=pltpu.CompilerParams(vmem_limit_bytes=60 * 1024 * 1024),
        name="net_sagittal" if halo else "net_coronal",
    )(x, current, cf, ch, cl)

def coronal_reflect(current, cf, ch, cl):
    slices, local, columns = current.shape
    strips = columns // local
    turned = jnp.transpose(current.reshape(slices, local, strips, local), (0, 3, 2, 1))
    t = turned.astype(BF)
    none = jnp.zeros((slices, 1, 1, local), BF)
    before = jnp.concatenate([none, t[:, -1:, :-1]], axis=2)
    after = jnp.concatenate([t[:, :1, 1:], none], axis=2)
    rest = jnp.zeros((slices, 6, strips, local), BF)
    x = jnp.concatenate([before, t, after, rest], axis=1)
    x = x.reshape(-1, columns)
    out = plane_call(2, x, turned.reshape(slices, local, columns), cf, ch, cl, 0, strips)
    return jnp.transpose(out.reshape(slices, local, strips, local), (0, 3, 2, 1)).reshape(current.shape)

def swap_halves(v):
    return pltpu.roll(v, 4, 0)

def block_pass(index_from, index_to, blocks, source, total, transposed, unroll=2):
    count = blocks.shape[0]
    low = lax.broadcasted_iota(jnp.int32, (8, LANES), 0) < 4
    zero = jnp.zeros((8, LANES), jnp.float32)

    def step(s, carry):
        b = s * 4
        picked = [source[index_from[b + j]] for j in range(4)]
        first = jnp.where(low, picked[0], picked[1])
        second = jnp.where(low, picked[2], picked[3])
        lhs = jnp.concatenate(
            [jnp.concatenate([first, zero], axis=0), jnp.concatenate([zero, second], axis=0)], axis=1
        ).astype(jnp.bfloat16)
        m = [blocks[b + j] for j in range(4)]
        if transposed:
            rhs = jnp.concatenate([jnp.concatenate([m[0], m[2]], axis=1), jnp.concatenate([m[1], m[3]], axis=1)], axis=0)
            y = lax.dot_general(lhs, rhs, (((1,), (1,)), ((), ())), preferred_element_type=jnp.float32)
        else:
            rhs = jnp.concatenate([jnp.concatenate([m[0], m[1]], axis=1), jnp.concatenate([m[2], m[3]], axis=1)], axis=0)
            y = jnp.dot(lhs, rhs, preferred_element_type=jnp.float32)
        parts = [
            jnp.where(low, y[:8, :LANES], 0.0),
            jnp.where(low, 0.0, y[:8, LANES:]),
            jnp.where(low, y[8:, :LANES], 0.0),
            jnp.where(low, 0.0, y[8:, LANES:]),
        ]
        for j in range(4):
            at = index_to[b + j]
            total[at] = total[at] + parts[j]
        return carry
    return step

def start_blocks(blocks_hbm, held, sems):
    n = blocks_hbm.shape[0] // CHUNK
    for i in range(n):
        pltpu.make_async_copy(blocks_hbm.at[pl.ds(i*CHUNK, CHUNK)], held.at[pl.ds(i*CHUNK, CHUNK)], sems.at[i]).start()

def wait_blocks(blocks_hbm, held, sems, i):
    pltpu.make_async_copy(blocks_hbm.at[pl.ds(i*CHUNK, CHUNK)], held.at[pl.ds(i*CHUNK, CHUNK)], sems.at[i]).wait()

def sweep(step, blocks_hbm, held, sems, waiting, unroll):
    n = held.shape[0] // CHUNK
    per = CHUNK // 4
    def chunk(i, c):
        if waiting:
            wait_blocks(blocks_hbm, held, sems, i)
        return lax.fori_loop(0, per // unroll, lambda s, c: functools.reduce(lambda c, u: step(i*per + s*unroll + u, c), range(unroll), c), c)
    lax.fori_loop(0, n, chunk, 0)

def compact(total, part_ref):
    low = lax.broadcasted_iota(jnp.int32, (8, LANES), 0) < 4
    pairs = total.shape[0] // 4
    def step(k, c):
        out = []
        for j in range(2):
            a = total[4*k + 2*j]; b = total[4*k + 2*j + 1]
            out.append(jnp.where(low, a + swap_halves(a), b + swap_halves(b)))
        part_ref[pl.ds(pl.multiple_of(16*k,16), 16)] = jnp.concatenate(out, axis=0).astype(jnp.bfloat16)
        return c
    lax.fori_loop(0, pairs, step, 0, unroll=4)

def expand(res_ref, spread):
    low = lax.broadcasted_iota(jnp.int32, (8, LANES), 0) < 4
    n = res_ref.shape[0] // 16
    def step(k, c):
        v = res_ref[pl.ds(pl.multiple_of(16*k,16), 16)].astype(jnp.float32)
        for j in range(2):
            u = v[8*j:8*j+8]
            w = swap_halves(u)
            spread[4*k + 2*j] = jnp.where(low, u, w)
            spread[4*k + 2*j + 1] = jnp.where(low, w, u)
        return c
    lax.fori_loop(0, n, step, 0, unroll=4)

def clear(ref, unroll=8):
    z = jnp.zeros((8,) + ref.shape[1:], ref.dtype)
    def step(i, c):
        ref[pl.ds(i*8, 8)] = z
        return c
    lax.fori_loop(0, ref.shape[0]//8, step, 0)

def project_kernel(rays, tiles, blocks_hbm, pixels, part_ref, held, total, sems):
    start_blocks(blocks_hbm, held, sems)
    clear(total)
    step = block_pass(tiles, rays, held, pixels, total, True)
    sweep(step, blocks_hbm, held, sems, True, UNROLL)
    compact(total, part_ref)

def back_update(rays, tiles, blocks_hbm, res_ref, pixels, moved_ref, held, spread, sems):
    start_blocks(blocks_hbm, held, sems)
    expand(res_ref, spread)
    clear(moved_ref)
    sweep(block_pass(rays, tiles, held, spread, moved_ref, False), blocks_hbm, held, sems, True, UNROLL)


def advance_kernel(rays, tiles, blocks_hbm, res_ref, pixels, part_ref, moved_ref, held, spread, total, sems):
    back_update(rays, tiles, blocks_hbm, res_ref, pixels, moved_ref, held, spread, sems)
    clear(total)

    def update(i, carry):
        at = pl.ds(i * 8, 8)
        a = moved_ref[at]
        moved_ref[at] = pixels[at] - 0.8 * (a + pltpu.roll(a, 4, 1))
        return carry

    lax.fori_loop(0, moved_ref.shape[0] // 8, update, 0)
    sweep(block_pass(tiles, rays, held, moved_ref, total, True), blocks_hbm, held, sems, False, UNROLL)
    compact(total, part_ref)


def settle_kernel(rays, tiles, blocks_hbm, res_ref, pixels, first_ref, out_ref, held, spread, sems):
    back_update(rays, tiles, blocks_hbm, res_ref, pixels, out_ref, held, spread, sems)

    def update(i, carry):
        at = pl.ds(i * 8, 8)
        a = out_ref[at]
        moved = pixels[at] - 0.8 * (a + pltpu.roll(a, 4, 1))
        out_ref[at] = 2.0 * moved - first_ref[at]
        return carry

    lax.fori_loop(0, out_ref.shape[0] // 8, update, 0)


def data_call(kernel, name, ins, outs, blocks, scratch):
    vmem = pl.BlockSpec(memory_space=pltpu.VMEM)
    smem = pl.BlockSpec(memory_space=pltpu.SMEM)
    anywhere = pl.BlockSpec(memory_space=pl.ANY)
    return pl.pallas_call(
        kernel,
        out_shape=outs,
        in_specs=[smem, smem, anywhere] + [vmem] * (len(ins) - 3),
        out_specs=jax.tree.map(lambda _: vmem, outs),
        scratch_shapes=[pltpu.VMEM(blocks.shape, BF)]
        + [pltpu.VMEM(s, F32) for s in scratch]
        + [pltpu.SemaphoreType.DMA((blocks.shape[0] // CHUNK,))],
        compiler_params=pltpu.CompilerParams(vmem_limit_bytes=40 * 1024 * 1024),
        name=name,
    )(*ins)


def halo_kernel(halo, cur_hbm, out_ref, edge, sent, load, send, recv):
    agent = lax.axis_index("agent")
    tile = lax.axis_index("tile")
    last = lax.axis_size("tile") - 1
    slices, local, columns = cur_hbm.shape
    rows = edge.shape[2]
    active = (agent == 1) | (agent == 2)

    def copy(side, peer):
        return pltpu.make_async_remote_copy(
            src_ref=sent.at[side],
            dst_ref=out_ref.at[1 - side],
            send_sem=send.at[side],
            recv_sem=recv.at[1 - side],
            device_id=(agent, peer),
            device_id_type=MESH,
        )

    @pl.when(active)
    def _():
        barrier = pltpu.get_barrier_semaphore()

        @pl.when(tile > 0)
        def _():
            pl.semaphore_signal(barrier, inc=1, device_id=(agent, tile - 1), device_id_type=MESH)

        @pl.when(tile < last)
        def _():
            pl.semaphore_signal(barrier, inc=1, device_id=(agent, tile + 1), device_id_type=MESH)

        loads = [
            pltpu.make_async_copy(cur_hbm.at[:, pl.ds(0, rows)], edge.at[0], load.at[0]),
            pltpu.make_async_copy(cur_hbm.at[:, pl.ds(local - rows, rows)], edge.at[1], load.at[1]),
        ]
        for item in loads:
            item.start()
        for item in loads:
            item.wait()
        for side in range(2):
            first = 0 if side == 0 else rows - halo
            parts = [edge[side, z, first:first + halo, :] for z in range(slices)]
            sent[side] = jnp.concatenate(parts, axis=0).astype(BF)

        pl.semaphore_wait(barrier, jnp.where(tile > 0, 1, 0) + jnp.where(tile < last, 1, 0))

        @pl.when(tile > 0)
        def _():
            copy(0, tile - 1).start()

        @pl.when(tile < last)
        def _():
            copy(1, tile + 1).start()

        @pl.when(tile == 0)
        def _():
            out_ref[0] = jnp.zeros(out_ref.shape[1:], BF)

        @pl.when(tile == last)
        def _():
            out_ref[1] = jnp.zeros(out_ref.shape[1:], BF)

        @pl.when(tile > 0)
        def _():
            copy(1, tile - 1).wait_recv()

        @pl.when(tile < last)
        def _():
            copy(0, tile + 1).wait_recv()

        @pl.when(tile > 0)
        def _():
            copy(0, tile - 1).wait_send()

        @pl.when(tile < last)
        def _():
            copy(1, tile + 1).wait_send()


def halo_exchange(current, halo):
    slices, local, columns = current.shape
    return pl.pallas_call(
        functools.partial(halo_kernel, halo),
        out_shape=jax.ShapeDtypeStruct((2, slices * halo, columns), BF),
        in_specs=[pl.BlockSpec(memory_space=pl.ANY)],
        out_specs=pl.BlockSpec(memory_space=pltpu.VMEM),
        scratch_shapes=[
            pltpu.VMEM((2, slices, 8, columns), F32),
            pltpu.VMEM((2, slices * halo, columns), BF),
            pltpu.SemaphoreType.DMA((2,)),
            pltpu.SemaphoreType.DMA((2,)),
            pltpu.SemaphoreType.DMA((2,)),
        ],
        compiler_params=pltpu.CompilerParams(collective_id=2, has_side_effects=True),
        name="halo_exchange",
    )(current)


def ray_kernel(count, part_ref, sino_ref, out_ref, got, fresh, send1, recv1, send2, recv2):
    rows = sino_ref.shape[0]
    agent = lax.axis_index("agent")

    @pl.when(agent == 0)
    def _():
        me = lax.axis_index("tile")
        barrier = pltpu.get_barrier_semaphore()
        for d in range(1, count):
            pl.semaphore_signal(barrier, inc=1, device_id=(agent, lax.rem(me + d, count)), device_id_type=MESH)
        pl.semaphore_wait(barrier, count - 1)

        def part_copy(d):
            peer = lax.rem(me + d, count)
            return pltpu.make_async_remote_copy(
                src_ref=part_ref.at[peer],
                dst_ref=got.at[d],
                send_sem=send1.at[d],
                recv_sem=recv1.at[d],
                device_id=(agent, peer),
                device_id_type=MESH,
            )

        for d in range(1, count):
            part_copy(d).start()
        total = part_ref[me].astype(jnp.float32) - sino_ref[...]
        for d in range(1, count):
            part_copy(d).wait_recv()
            total = total + got[d].astype(jnp.float32)
        fresh[...] = total.astype(jnp.bfloat16)

        def rest_copy(d):
            return pltpu.make_async_remote_copy(
                src_ref=fresh,
                dst_ref=got2_slot(me),
                send_sem=send2.at[d],
                recv_sem=recv2.at[d],
                device_id=(agent, lax.rem(me + d, count)),
                device_id_type=MESH,
            )

        def got2_slot(slot):
            return out_ref.at[slot]

        for d in range(1, count):
            rest_copy(d).start()
        out_ref[me] = fresh[...]
        for d in range(1, count):
            rest_copy(d).wait_recv()
        for d in range(1, count):
            part_copy(d).wait_send()
            rest_copy(d).wait_send()


def ray_exchange(part, sinogram, count):
    rows = sinogram.shape[0]
    whole = pl.BlockSpec(memory_space=pltpu.VMEM)
    return pl.pallas_call(
        functools.partial(ray_kernel, count),
        out_shape=jax.ShapeDtypeStruct((count, rows, LANES), jnp.bfloat16),
        in_specs=[whole] * 2,
        out_specs=whole,
        scratch_shapes=[
            pltpu.VMEM((count, rows, LANES), jnp.bfloat16),
            pltpu.VMEM((rows, LANES), jnp.bfloat16),
            pltpu.SemaphoreType.DMA((count,)),
            pltpu.SemaphoreType.DMA((count,)),
            pltpu.SemaphoreType.DMA((count,)),
            pltpu.SemaphoreType.DMA((count,)),
        ],
        compiler_params=pltpu.CompilerParams(collective_id=0, has_side_effects=True),
        name="ray_exchange",
    )(part, sinogram)


def agent_kernel(own_ref, out_ref, near, pair, far, send, recv):
    me = lax.axis_index("agent")
    tile = lax.axis_index("tile")
    partner = me + 1 - 2 * (me % 2)
    across = (me + 2) % 4
    barrier = pltpu.get_barrier_semaphore()
    for peer in (partner, across):
        pl.semaphore_signal(barrier, inc=1, device_id=(peer, tile), device_id_type=MESH)
    pl.semaphore_wait(barrier, 2)

    first = pltpu.make_async_remote_copy(
        src_ref=own_ref,
        dst_ref=near,
        send_sem=send.at[0],
        recv_sem=recv.at[0],
        device_id=(partner, tile),
        device_id_type=MESH,
    )
    first.start()
    first.wait()
    pair[...] = (own_ref[...].astype(jnp.float32) + near[...].astype(jnp.float32)).astype(jnp.bfloat16)
    second = pltpu.make_async_remote_copy(
        src_ref=pair,
        dst_ref=far,
        send_sem=send.at[1],
        recv_sem=recv.at[1],
        device_id=(across, tile),
        device_id_type=MESH,
    )
    second.start()
    second.wait()
    out_ref[...] = near[...].astype(jnp.float32) + far[...].astype(jnp.float32)


def agent_sum(own):
    whole = pl.BlockSpec(memory_space=pltpu.VMEM)
    return pl.pallas_call(
        agent_kernel,
        out_shape=jax.ShapeDtypeStruct(own.shape, jnp.float32),
        in_specs=[whole],
        out_specs=whole,
        scratch_shapes=[
            pltpu.VMEM(own.shape, jnp.bfloat16),
            pltpu.VMEM(own.shape, jnp.bfloat16),
            pltpu.VMEM(own.shape, jnp.bfloat16),
            pltpu.SemaphoreType.DMA((2,)),
            pltpu.SemaphoreType.DMA((2,)),
        ],
        compiler_params=pltpu.CompilerParams(collective_id=1, has_side_effects=True),
        name="agent_sum",
    )(own)


def per_device(
    states,
    sinogram,
    blocks,
    block_angle,
    block_detector,
    block_tile,
    conv_first,
    conv_hidden,
    conv_last,
):
    current = states[0]
    slices, local_rows, image_columns = current.shape
    tile_count = lax.axis_size("tile")
    agent_place = lax.axis_index("agent")
    is_data = agent_place == 0
    tiles_here = local_rows * image_columns // LANES
    rays_here = sinogram.shape[0]
    ray_total = rays_here * tile_count
    part_shape = (tile_count, rays_here * slices, LANES)
    halo = conv_hidden.shape[1] + 2
    filters = (conv_first, conv_hidden, conv_last)
    rays = block_angle * (image_columns // LANES) + block_detector
    pixel_shape = jax.ShapeDtypeStruct((tiles_here, 2 * slices, LANES), F32)
    part_type = jax.ShapeDtypeStruct((ray_total * slices, LANES), BF)
    ray_shape = (ray_total, 2 * slices, LANES)

    def tiled():
        pixels = jnp.transpose(current.reshape(slices, tiles_here, LANES), (1, 0, 2))
        return jnp.concatenate([pixels, pixels], axis=1)

    edges = halo_exchange(current, halo)
    no_part = jnp.zeros(part_shape, BF)
    no_pixels = jnp.zeros(pixel_shape.shape, F32)

    def data_start():
        pixels = tiled()
        part = data_call(project_kernel, "project", (rays, block_tile, blocks, pixels), part_type, blocks, [ray_shape])
        return part.reshape(part_shape), pixels, current

    def axial_only():
        return no_part, no_pixels, axial_reflect(edges, current, *filters, halo)

    def sagittal_only():
        return no_part, no_pixels, plane_call(1, edges, current, *filters, halo, 1)

    def coronal_only():
        return no_part, no_pixels, coronal_reflect(current, *filters)

    part, pixels, reflect = lax.switch(agent_place, [data_start, axial_only, sagittal_only, coronal_only])
    own_sinogram = sinogram.reshape(rays_here * slices, LANES)
    first = pixels

    for step in range(DATA_STEPS):
        residual = ray_exchange(part, own_sinogram, tile_count)
        if step < DATA_STEPS - 1:

            def advance(pixels, residual):
                ins = (rays, block_tile, blocks, residual.reshape(part_type.shape), pixels)
                part, moved = data_call(
                    advance_kernel, "advance", ins, (part_type, pixel_shape), blocks, [ray_shape, ray_shape]
                )
                return part.reshape(part_shape), moved

            part, pixels = lax.cond(is_data, advance, lambda p, r: (no_part, p), pixels, residual)
        else:

            def settle(pixels, first, reflect, residual):
                ins = (rays, block_tile, blocks, residual.reshape(part_type.shape), pixels, first)
                out = data_call(settle_kernel, "settle", ins, pixel_shape, blocks, [ray_shape])
                return jnp.transpose(out[:, :slices], (1, 0, 2)).reshape(reflect.shape)

            reflect = lax.cond(is_data, settle, lambda p, f, s, r: s, pixels, first, reflect, residual)

    sent = reflect.astype(BF).reshape(slices * local_rows, image_columns)
    others = agent_sum(sent).reshape(reflect.shape)
    new_states = 0.5 * current + 0.25 * others - 0.25 * reflect
    return new_states[None]


def solution(mesh):
    placed = (
        P("agent", None, "tile", None),
        P("tile", None, None),
        P("tile", None, None),
        P("tile"),
        P("tile"),
        P("tile"),
        P(),
        P(),
        P(),
    )
    return jax.shard_map(
        per_device,
        mesh=mesh,
        in_specs=placed,
        out_specs=P("agent", None, "tile", None),
        check_vma=False,
    )
```

time: 102 us -> 68.5 us (0.67)
  matrix products: 30.3 us -> 0 us
  Pallas kernels: 49.5 us -> 62.2 us
  starting transfers between devices: 6.19 us -> 0 us
  other arithmetic: 9.3 us -> 3.65 us
  waiting for transfers between devices: 4.32 us -> 0 us
    dot_general x12 -> x0, matrix products: 30.3 us -> none  [the longest x2 15.6 us: project(): jnp.einsum('bzp,bqp->bzq', picked, blocks, preferred_element_type=jnp.flo...]
    pallas_call x0 -> x4, Pallas kernels: none -> 18.6 us  [the longest x3 18.5 us: data_call(): pl.pallas_call(kernel, out_shape=outs, in_specs=[smem, smem, anywhere] +...]
    pallas_call x1, Pallas kernels: 19.4 us -> 11.9 us  [agent_sum(): pl.pallas_call(agent_kernel, out_shape=jax.ShapeDtypeStruct(own.shape, jn...]
    ppermute x2 -> x0, starting transfers between devices: 6.19 us -> none  [the longest x1 4.9 us: extended(): lax.ppermute(tail, axis, [(i, (i + 1) % count) for i in range(ends)])]
    convert_element_type x4 -> x1, other arithmetic: 5.29 us -> 0.74 us  [per_device(): sent = reflect.astype(BF).reshape(slices * local_rows, image_columns)]
    ppermute x2 -> x0, waiting for transfers between devices: 4.32 us -> none  [the longest x1 4.21 us: extended(): lax.ppermute(head, axis, [((i + 1) % count, i) for i in range(ends)])]
    pallas_call x2, Pallas kernels: 30.1 us -> 31.7 us  [ray_exchange(): pl.pallas_call(functools.partial(ray_kernel, count), out_shape=jax.ShapeD...]
    another operation x0 -> x2, local copies, waits for them, and re-layouts: none -> 1.42 us  [tiled(): current.reshape(slices, tiles_here, LANES)]
  transfers between devices with their start and end apart: 2 -> 0, of which waited for: 2 -> 0; matrix products, arithmetic and copies ran while one was open for 0% -> 0% of each run, Pallas kernels for 0% -> 0%
where the time goes in v1:
time: 68.5 us; the launch traced here: 68.1 us
  Pallas kernels  62.2 us (91%)
  other arithmetic  3.65 us (5%)
  local copies, waits for them, and re-layouts  1.79 us (3%)
    pallas_call x2, Pallas kernels, ray_exchange(): pl.pallas_call(functools.partial(ray_kernel, count), out_shape=jax.ShapeD...  31.7 us
    pallas_call x3, Pallas kernels, data_call(): pl.pallas_call(kernel, out_shape=outs, in_specs=[smem, smem, anywhere] +...  18.5 us
    pallas_call x1, Pallas kernels, agent_sum(): pl.pallas_call(agent_kernel, out_shape=jax.ShapeDtypeStruct(own.shape, jn...  11.9 us
    another operation x2, local copies, waits for them, and re-layouts, tiled(): current.reshape(slices, tiles_here, LANES)  1.42 us

profile of v1, /device:TPU:0, one launch (start us, length us, event | category | flops | bytes accessed | tf_op | source)
XLA Modules:
  0.0 68.1 jit_solution(7154599695436775370)
XLA Ops:
  0.0 0.7 %multiply_add_fusion = s32[256]{0:T(256)S(1)} fusion(s32[256]{0:T(256)} %param.21, s32[256]{0:T(256)} %param.20), kind=kLoop, calls=%fused_computation.15 | loop fusion | flops 512 | bytes 3072 | tf_op jit(solution)/shard_map/add | solution.py:821
  0.7 0.1 halo_exchange.1
  0.8 7.4 %conditional.3 = (bf16[8,128,128]{2,1,0:T(8,128)(2,1)S(1)}, f32[256,8,128]{2,1,0:T(8,128)S(1)}, f32[4,64,512]{2,1,0:T(8,128)S(1)}) conditional(s32[]{:T(128)} %clamp.3, (f32[1,4,64,512]{3,2,1,0:T(8,128)}, s32[256]{0:T(256)S(1)}, s32[256]{0:T(256)}, bf16[256,128,128]{2,1,0:T(8,128)(2,1)}, ...), branch_computations={%region_0.0_spmd, %region_1.0_spmd, %region_2.0_spmd, %region_3.0_... | conditional | flops 2195456 | bytes 10013614 | solution.py:848
  0.8 1.1 %reshape_squeeze.4 = f32[4,256,128]{2,1,0:T(8,128)S(1)} reshape(f32[1,4,64,512]{3,2,1,0:T(8,128)} %bitcast.33) | data formatting | bytes 1048576 | tf_op jit(solution)/shard_map/cond/branch_0_fun/reshape;squeeze | solution.py:827
  1.9 0.0 copy-start.5
  1.9 0.3 copy.17
  2.2 0.2 pad_maximum_fusion.pixels
  2.4 0.1 copy-done.5
  2.5 5.3 %project.1 = bf16[1024,128]{1,0:T(8,128)(2,1)S(1)} custom-call(s32[256]{0:T(256)S(1)} %get-tuple-element.70.rays, s32[256]{0:T(256)S(1)} %copy-done.5, bf16[256,128,128]{2,1,0:T(8,128)(2,1)} %get-tuple-element.72.blocks_hbm, f32[256,8,128]{2,1,0:T(8,128)S(1)} %pad_maximum_fusion.pixels), custom_call_target="tpu_custom_call" | custom-call | tf_op jit(solution)/shard_map/cond/branch_0_fun/project/pallas_call | solution.py:561
  7.9 0.0 copy-done.1
  8.1 17.5 %ray_exchange.2 = bf16[8,128,128]{2,1,0:T(8,128)(2,1)S(1)} custom-call(bf16[8,128,128]{2,1,0:T(8,128)(2,1)S(1)} %get-tuple-element.109.part_ref, f32[128,128]{1,0:T(8,128)} %bitcast.43), custom_call_target="tpu_custom_call" | custom-call | tf_op jit(solution)/shard_map/ray_exchange/pallas_call | solution.py:728
  25.6 8.4 %conditional.4 = (bf16[8,128,128]{2,1,0:T(8,128)(2,1)S(1)}, f32[256,8,128]{2,1,0:T(8,128)S(1)}) conditional(s32[]{:T(128)} %convert_element_type.10, f32[256,8,128]{2,1,0:T(8,128)S(1)} %get-tuple-element.108, (bf16[8,128,128]{2,1,0:T(8,128)(2,1)S(1)}, s32[256]{0:T(256)S(1)}, s32[256]{0:T(256)}, bf16[256,128,128]{2,1,0:T(8,128)(2,1)}, ...), branch_computations={%region_4.0_spmd, %region_5.0_spmd} | conditional | bytes 2359314 | solution.py:863
  25.6 8.4 %advance.1 = (bf16[1024,128]{1,0:T(8,128)(2,1)S(1)}, f32[256,8,128]{2,1,0:T(8,128)S(1)}) custom-call(s32[256]{0:T(256)S(1)} %get-tuple-element.89.rays, s32[256]{0:T(256)} %get-tuple-element.90.tiles, bf16[256,128,128]{2,1,0:T(8,128)(2,1)} %get-tuple-element.91.blocks_hbm, bf16[1024,128]{1,0:T(8,128)(2,1)S(1)} %bitcast.41, ...), custom_call_target="tpu_custom_call" | custom-call | tf_op jit(solution)/shard_map/cond/branch_1_fun/advance/pallas_call | solution.py:561
  34.0 14.3 %ray_exchange.3 = bf16[8,128,128]{2,1,0:T(8,128)(2,1)S(1)} custom-call(bf16[8,128,128]{2,1,0:T(8,128)(2,1)S(1)} %get-tuple-element.110.part_ref, f32[128,128]{1,0:T(8,128)} %bitcast.44), custom_call_target="tpu_custom_call" | custom-call | tf_op jit(solution)/shard_map/ray_exchange/pallas_call | solution.py:728
  48.3 5.1 %conditional.5 = (f32[4,64,512]{2,1,0:T(8,128)S(1)}) conditional(s32[]{:T(128)} %convert_element_type.10, f32[4,64,512]{2,1,0:T(8,128)S(1)} %get-tuple-element.107, (bf16[8,128,128]{2,1,0:T(8,128)(2,1)S(1)}, s32[256]{0:T(256)S(1)}, s32[256]{0:T(256)}, bf16[256,128,128]{2,1,0:T(8,128)(2,1)}, f32[256,8,128]{2,1,0:T(8,128)S(1)}, ...), branch_computations={%region_6.0_spmd, %region_7.0_spmd} | conditional | bytes 3145736 | solution.py:871
  48.3 4.9 %settle.1 = f32[256,8,128]{2,1,0:T(8,128)S(1)} custom-call(s32[256]{0:T(256)S(1)} %get-tuple-element.96.rays, s32[256]{0:T(256)} %get-tuple-element.97.tiles, bf16[256,128,128]{2,1,0:T(8,128)(2,1)} %get-tuple-element.98.blocks_hbm, bf16[1024,128]{1,0:T(8,128)(2,1)S(1)} %bitcast.39, f32[256,8,128]{2,1,0:T(8,128)S(1)} %get-tuple-element.100.pixels, ...), custom_call_target="tpu_custom_call" | custom-call | tf_op jit(solution)/shard_map/cond/branch_1_fun/settle/pallas_call | solution.py:561
  53.2 0.1 slice_bitcast_fusion
  53.3 0.1 reshape.33
  53.4 0.0 copy-start
  53.4 0.7 %convert_element_type.11 = bf16[4,64,512]{2,1,0:T(8,128)(2,1)} convert(f32[4,64,512]{2,1,0:T(8,128)S(1)} %get-tuple-element.130) | non-fusion elementwise | flops 131072 | bytes 786432 | tf_op jit(solution)/shard_map/convert_element_type | solution.py:873
  54.1 11.9 %agent_sum.1 = f32[256,512]{1,0:T(8,128)} custom-call(bf16[256,512]{1,0:T(8,128)(2,1)} %bitcast.38), custom_call_target="tpu_custom_call" | custom-call | tf_op jit(solution)/shard_map/agent_sum/pallas_call | solution.py:782
  66.0 1.1 %broadcast_multiply_fusion = f32[256,512]{1,0:T(8,128)S(1)} fusion(f32[256,512]{1,0:T(8,128)} %agent_sum.1), kind=kLoop, calls=%fused_computation.14 | loop fusion | flops 131072 | bytes 1048576 | tf_op jit(solution)/shard_map/mul | solution.py:875
  67.1 0.0 copy-done
  67.1 1.0 %subtract_bitcast_fusion = f32[1,4,64,512]{3,2,1,0:T(8,128)} fusion(f32[4,64,512]{2,1,0:T(8,128)S(1)} %get-tuple-element.130, f32[4,64,512]{2,1,0:T(8,128)S(1)} %bitcast.37, f32[1,4,64,512]{3,2,1,0:T(8,128)S(1)} %copy-done), kind=kLoop, calls=%fused_computation.13 | loop fusion | flops 524288 | bytes 2097152 | tf_op jit(solution)/shard_map/broadcast_in_dim | solution.py:876
  (3 shorter events, 0.1 us)
Async XLA Ops:
  1.9 0.7 %copy-start.5 = (s32[256]{0:T(256)S(1)}, s32[256]{0:T(256)}, u32[]{:S(2)}) copy-start(s32[256]{0:T(256)} %get-tuple-element.71.tiles) | copy-start | bytes 3076 | tf_op jit(solution)/shard_map/cond
  2.5 5.3 %copy-start.1 = (f32[4,64,512]{2,1,0:T(8,128)S(1)}, f32[4,64,512]{2,1,0:T(8,128)}, u32[]{:S(2)}) copy-start(f32[4,64,512]{2,1,0:T(8,128)} %get-tuple-element.116) | copy-start | bytes 1572868 | tf_op jit(solution)/shard_map/cond
  53.4 13.8 %copy-start = (f32[1,4,64,512]{3,2,1,0:T(8,128)S(1)}, f32[1,4,64,512]{3,2,1,0:T(8,128)}, u32[]{:S(2)}) copy-start(f32[1,4,64,512]{3,2,1,0:T(8,128)} %param.17) | copy-start | bytes 1572868

commit v2 on v1

--- a/solution.py
+++ b/solution.py
@@ -12,7 +12,6 @@
 LANES = 128
 STRIPS = 16
 CHUNK = 32
-UNROLL = 8
 BF = jnp.bfloat16
 F32 = jnp.float32
 NATURAL = (0, 1, 2, 3)
@@ -428,149 +427,6 @@
     out = plane_call(2, x, turned.reshape(slices, local, columns), cf, ch, cl, 0, strips)
     return jnp.transpose(out.reshape(slices, local, strips, local), (0, 3, 2, 1)).reshape(current.shape)
 
-def swap_halves(v):
-    return pltpu.roll(v, 4, 0)
-
-def block_pass(index_from, index_to, blocks, source, total, transposed, unroll=2):
-    count = blocks.shape[0]
-    low = lax.broadcasted_iota(jnp.int32, (8, LANES), 0) < 4
-    zero = jnp.zeros((8, LANES), jnp.float32)
-
-    def step(s, carry):
-        b = s * 4
-        picked = [source[index_from[b + j]] for j in range(4)]
-        first = jnp.where(low, picked[0], picked[1])
-        second = jnp.where(low, picked[2], picked[3])
-        lhs = jnp.concatenate(
-            [jnp.concatenate([first, zero], axis=0), jnp.concatenate([zero, second], axis=0)], axis=1
-        ).astype(jnp.bfloat16)
-        m = [blocks[b + j] for j in range(4)]
-        if transposed:
-            rhs = jnp.concatenate([jnp.concatenate([m[0], m[2]], axis=1), jnp.concatenate([m[1], m[3]], axis=1)], axis=0)
-            y = lax.dot_general(lhs, rhs, (((1,), (1,)), ((), ())), preferred_element_type=jnp.float32)
-        else:
-            rhs = jnp.concatenate([jnp.concatenate([m[0], m[1]], axis=1), jnp.concatenate([m[2], m[3]], axis=1)], axis=0)
-            y = jnp.dot(lhs, rhs, preferred_element_type=jnp.float32)
-        parts = [
-            jnp.where(low, y[:8, :LANES], 0.0),
-            jnp.where(low, 0.0, y[:8, LANES:]),
-            jnp.where(low, y[8:, :LANES], 0.0),
-            jnp.where(low, 0.0, y[8:, LANES:]),
-        ]
-        for j in range(4):
-            at = index_to[b + j]
-            total[at] = total[at] + parts[j]
-        return carry
-    return step
-
-def start_blocks(blocks_hbm, held, sems):
-    n = blocks_hbm.shape[0] // CHUNK
-    for i in range(n):
-        pltpu.make_async_copy(blocks_hbm.at[pl.ds(i*CHUNK, CHUNK)], held.at[pl.ds(i*CHUNK, CHUNK)], sems.at[i]).start()
-
-def wait_blocks(blocks_hbm, held, sems, i):
-    pltpu.make_async_copy(blocks_hbm.at[pl.ds(i*CHUNK, CHUNK)], held.at[pl.ds(i*CHUNK, CHUNK)], sems.at[i]).wait()
-
-def sweep(step, blocks_hbm, held, sems, waiting, unroll):
-    n = held.shape[0] // CHUNK
-    per = CHUNK // 4
-    def chunk(i, c):
-        if waiting:
-            wait_blocks(blocks_hbm, held, sems, i)
-        return lax.fori_loop(0, per // unroll, lambda s, c: functools.reduce(lambda c, u: step(i*per + s*unroll + u, c), range(unroll), c), c)
-    lax.fori_loop(0, n, chunk, 0)
-
-def compact(total, part_ref):
-    low = lax.broadcasted_iota(jnp.int32, (8, LANES), 0) < 4
-    pairs = total.shape[0] // 4
-    def step(k, c):
-        out = []
-        for j in range(2):
-            a = total[4*k + 2*j]; b = total[4*k + 2*j + 1]
-            out.append(jnp.where(low, a + swap_halves(a), b + swap_halves(b)))
-        part_ref[pl.ds(pl.multiple_of(16*k,16), 16)] = jnp.concatenate(out, axis=0).astype(jnp.bfloat16)
-        return c
-    lax.fori_loop(0, pairs, step, 0, unroll=4)
-
-def expand(res_ref, spread):
-    low = lax.broadcasted_iota(jnp.int32, (8, LANES), 0) < 4
-    n = res_ref.shape[0] // 16
-    def step(k, c):
-        v = res_ref[pl.ds(pl.multiple_of(16*k,16), 16)].astype(jnp.float32)
-        for j in range(2):
-            u = v[8*j:8*j+8]
-            w = swap_halves(u)
-            spread[4*k + 2*j] = jnp.where(low, u, w)
-            spread[4*k + 2*j + 1] = jnp.where(low, w, u)
-        return c
-    lax.fori_loop(0, n, step, 0, unroll=4)
-
-def clear(ref, unroll=8):
-    z = jnp.zeros((8,) + ref.shape[1:], ref.dtype)
-    def step(i, c):
-        ref[pl.ds(i*8, 8)] = z
-        return c
-    lax.fori_loop(0, ref.shape[0]//8, step, 0)
-
-def project_kernel(rays, tiles, blocks_hbm, pixels, part_ref, held, total, sems):
-    start_blocks(blocks_hbm, held, sems)
-    clear(total)
-    step = block_pass(tiles, rays, held, pixels, total, True)
-    sweep(step, blocks_hbm, held, sems, True, UNROLL)
-    compact(total, part_ref)
-
-def back_update(rays, tiles, blocks_hbm, res_ref, pixels, moved_ref, held, spread, sems):
-    start_blocks(blocks_hbm, held, sems)
-    expand(res_ref, spread)
-    clear(moved_ref)
-    sweep(block_pass(rays, tiles, held, spread, moved_ref, False), blocks_hbm, held, sems, True, UNROLL)
-
-
-def advance_kernel(rays, tiles, blocks_hbm, res_ref, pixels, part_ref, moved_ref, held, spread, total, sems):
-    back_update(rays, tiles, blocks_hbm, res_ref, pixels, moved_ref, held, spread, sems)
-    clear(total)
-
-    def update(i, carry):
-        at = pl.ds(i * 8, 8)
-        a = moved_ref[at]
-        moved_ref[at] = pixels[at] - 0.8 * (a + pltpu.roll(a, 4, 1))
-        return carry
-
-    lax.fori_loop(0, moved_ref.shape[0] // 8, update, 0)
-    sweep(block_pass(tiles, rays, held, moved_ref, total, True), blocks_hbm, held, sems, False, UNROLL)
-    compact(total, part_ref)
-
-
-def settle_kernel(rays, tiles, blocks_hbm, res_ref, pixels, first_ref, out_ref, held, spread, sems):
-    back_update(rays, tiles, blocks_hbm, res_ref, pixels, out_ref, held, spread, sems)
-
-    def update(i, carry):
-        at = pl.ds(i * 8, 8)
-        a = out_ref[at]
-        moved = pixels[at] - 0.8 * (a + pltpu.roll(a, 4, 1))
-        out_ref[at] = 2.0 * moved - first_ref[at]
-        return carry
-
-    lax.fori_loop(0, out_ref.shape[0] // 8, update, 0)
-
-
-def data_call(kernel, name, ins, outs, blocks, scratch):
-    vmem = pl.BlockSpec(memory_space=pltpu.VMEM)
-    smem = pl.BlockSpec(memory_space=pltpu.SMEM)
-    anywhere = pl.BlockSpec(memory_space=pl.ANY)
-    return pl.pallas_call(
-        kernel,
-        out_shape=outs,
-        in_specs=[smem, smem, anywhere] + [vmem] * (len(ins) - 3),
-        out_specs=jax.tree.map(lambda _: vmem, outs),
-        scratch_shapes=[pltpu.VMEM(blocks.shape, BF)]
-        + [pltpu.VMEM(s, F32) for s in scratch]
-        + [pltpu.SemaphoreType.DMA((blocks.shape[0] // CHUNK,))],
-        compiler_params=pltpu.CompilerParams(vmem_limit_bytes=40 * 1024 * 1024),
-        name=name,
-    )(*ins)
-
-
 def halo_kernel(halo, cur_hbm, out_ref, edge, sent, load, send, recv):
     agent = lax.axis_index("agent")
     tile = lax.axis_index("tile")
@@ -668,132 +524,302 @@
     )(current)
 
 
-def ray_kernel(count, part_ref, sino_ref, out_ref, got, fresh, send1, recv1, send2, recv2):
-    rows = sino_ref.shape[0]
+def swap_bits(me, d):
+    peer, bit = me, 1
+    while bit <= d:
+        if d & bit:
+            peer = peer + bit * (1 - 2 * ((me // bit) % 2))
+        bit *= 2
+    return peer
+
+
+def block_copy(blocks_hbm, held, sems, i):
+    at = pl.ds(i * CHUNK, CHUNK)
+    return pltpu.make_async_copy(blocks_hbm.at[at], held.at[at], sems.at[i])
+
+
+def block_step(held, picked, y, slices, transposed, u):
+    row = lax.broadcasted_iota(jnp.int32, (8, LANES), 0)
+    at = pl.ds(pl.multiple_of(8 * u, 8), 8)
+    p = [picked[at, z * LANES:(z + 1) * LANES] for z in range(slices)]
+    halves = []
+    for t in range(2):
+        sides = []
+        for side in range(2):
+            mask = row // 2 == 2 * t + side
+            sides.append(jnp.concatenate([jnp.where(mask, v, 0.0) for v in p], axis=0))
+        lhs = jnp.concatenate(sides, axis=1).astype(BF)
+        m = [held[8 * u + 4 * t + j] for j in range(4)]
+        if transposed:
+            top, bottom = jnp.concatenate([m[0], m[2]], axis=1), jnp.concatenate([m[1], m[3]], axis=1)
+            dims = (((1,), (1,)), ((), ()))
+        else:
+            top, bottom = jnp.concatenate([m[0], m[1]], axis=1), jnp.concatenate([m[2], m[3]], axis=1)
+            dims = (((1,), (0,)), ((), ()))
+        rhs = jnp.concatenate([top, bottom], axis=0)
+        halves.append(lax.dot_general(lhs, rhs, dims, preferred_element_type=F32))
+    for z in range(slices):
+        a, b = (h[8 * z:8 * z + 8] for h in halves)
+        low = jnp.where(row < 4, a[:, :LANES], b[:, :LANES])
+        high = jnp.where(row < 4, a[:, LANES:], b[:, LANES:])
+        y[at, z * LANES:(z + 1) * LANES] = jnp.where(row % 2 == 0, low, high)
+
+
+def block_sweep(blocks_hbm, held, sems, picked, y, slices, transposed, waiting):
+    def chunk(i, carry):
+        if waiting:
+            block_copy(blocks_hbm, held, sems, i).wait()
+        for j in range(CHUNK // 8):
+            block_step(held, picked, y, slices, transposed, i * (CHUNK // 8) + j)
+        return carry
+
+    lax.fori_loop(0, held.shape[0] // CHUNK, chunk, 0)
+
+
+def gather_rows(hot, source):
+    return jnp.dot(hot, source, preferred_element_type=F32)
+
+
+def scatter_rows(hot, y):
+    high = y.astype(BF)
+    low = (y - high.astype(F32)).astype(BF)
+    return jnp.dot(
+        jnp.concatenate([hot, hot], axis=1), jnp.concatenate([high, low], axis=0), preferred_element_type=F32
+    )
+
+
+def data_kernel(
+    count, angle_ref, detector_ref, tile_ref, sino_ref, cur_hbm, blocks_hbm, out_ref,
+    held, cur, ray_hot, ray_turned, tile_hot, tile_turned, x, y, picked, total, part, got, fresh, full,
+    load, sems, send1, recv1, send2, recv2,
+):
     agent = lax.axis_index("agent")
+    me = lax.axis_index("tile")
+    slices, local, columns = out_ref.shape
+    detectors = columns // LANES
+    rays_here = fresh.shape[1]
+    ray_total = count * rays_here
+    tiles_here = detectors * local
+    blocks_here = held.shape[0]
+    order = list(range(count - 1, 0, -1))
+
+    def part_copy(step, d):
+        return pltpu.make_async_remote_copy(
+            src_ref=part.at[step, swap_bits(me, d)],
+            dst_ref=got.at[step, d],
+            send_sem=send1.at[step, d],
+            recv_sem=recv1.at[step, d],
+            device_id=(agent, swap_bits(me, d)),
+            device_id_type=MESH,
+        )
+
+    def rest_copy(step, d):
+        return pltpu.make_async_remote_copy(
+            src_ref=fresh.at[step],
+            dst_ref=full.at[step, me],
+            send_sem=send2.at[step, d],
+            recv_sem=recv2.at[step, d],
+            device_id=(agent, swap_bits(me, d)),
+            device_id_type=MESH,
+        )
+
+    def exchange(step):
+        for slot in range(count):
+            part[step, slot] = total[slot * rays_here:(slot + 1) * rays_here, :].astype(BF)
+        for d in order:
+            part_copy(step, d).start()
+        own = total[pl.ds(pl.multiple_of(me * rays_here, 8), rays_here), :]
+        measured = [sino_ref[pl.ds(z, rays_here, stride=slices), :] for z in range(slices)]
+        value = own - jnp.concatenate(measured, axis=1)
+        for d in reversed(order):
+            part_copy(step, d).wait_recv()
+            value = value + got[step, d].astype(F32)
+        fresh[step] = value.astype(BF)
+        for d in order:
+            rest_copy(step, d).start()
+        full[step, me] = fresh[step]
+        for d in order:
+            rest_copy(step, d).wait_recv()
+        for d in order:
+            part_copy(step, d).wait_send()
+            rest_copy(step, d).wait_send()
+        return full[step].reshape(ray_total, slices * LANES)
 
     @pl.when(agent == 0)
     def _():
-        me = lax.axis_index("tile")
         barrier = pltpu.get_barrier_semaphore()
-        for d in range(1, count):
-            pl.semaphore_signal(barrier, inc=1, device_id=(agent, lax.rem(me + d, count)), device_id_type=MESH)
-        pl.semaphore_wait(barrier, count - 1)
-
-        def part_copy(d):
-            peer = lax.rem(me + d, count)
-            return pltpu.make_async_remote_copy(
-                src_ref=part_ref.at[peer],
-                dst_ref=got.at[d],
-                send_sem=send1.at[d],
-                recv_sem=recv1.at[d],
-                device_id=(agent, peer),
-                device_id_type=MESH,
-            )
-
-        for d in range(1, count):
-            part_copy(d).start()
-        total = part_ref[me].astype(jnp.float32) - sino_ref[...]
-        for d in range(1, count):
-            part_copy(d).wait_recv()
-            total = total + got[d].astype(jnp.float32)
-        fresh[...] = total.astype(jnp.bfloat16)
-
-        def rest_copy(d):
-            return pltpu.make_async_remote_copy(
-                src_ref=fresh,
-                dst_ref=got2_slot(me),
-                send_sem=send2.at[d],
-                recv_sem=recv2.at[d],
-                device_id=(agent, lax.rem(me + d, count)),
-                device_id_type=MESH,
-            )
-
-        def got2_slot(slot):
-            return out_ref.at[slot]
-
-        for d in range(1, count):
-            rest_copy(d).start()
-        out_ref[me] = fresh[...]
-        for d in range(1, count):
-            rest_copy(d).wait_recv()
-        for d in range(1, count):
-            part_copy(d).wait_send()
-            rest_copy(d).wait_send()
-
-
-def ray_exchange(part, sinogram, count):
-    rows = sinogram.shape[0]
-    whole = pl.BlockSpec(memory_space=pltpu.VMEM)
+        for d in order:
+            pl.semaphore_signal(barrier, inc=1, device_id=(agent, swap_bits(me, d)), device_id_type=MESH)
+        first = pltpu.make_async_copy(cur_hbm, cur, load.at[0])
+        first.start()
+        for i in range(blocks_here // CHUNK):
+            block_copy(blocks_hbm, held, sems, i).start()
+
+        hot_rows = lax.broadcasted_iota(jnp.int32, (ray_total, blocks_here), 0)
+        ray = angle_ref[...] * detectors + detector_ref[...]
+        hot = jnp.where(hot_rows == jnp.broadcast_to(ray, hot_rows.shape), 1.0, 0.0)
+        ray_hot[...] = hot.astype(BF)
+        ray_turned[...] = hot.T.astype(BF)
+        hot_rows = lax.broadcasted_iota(jnp.int32, (tiles_here, blocks_here), 0)
+        place = tile_ref[...]
+        place = (place % detectors) * local + place // detectors
+        hot = jnp.where(hot_rows == jnp.broadcast_to(place, hot_rows.shape), 1.0, 0.0)
+        tile_hot[...] = hot.astype(BF)
+        tile_turned[...] = hot.T.astype(BF)
+
+        first.wait()
+        for z in range(slices):
+            for t in range(detectors):
+                x[t * local:(t + 1) * local, z * LANES:(z + 1) * LANES] = cur[z, :, t * LANES:(t + 1) * LANES]
+
+        for step in range(DATA_STEPS):
+            picked[...] = gather_rows(tile_turned[...], x[...].astype(BF))
+            block_sweep(blocks_hbm, held, sems, picked, y, slices, True, step == 0)
+            total[...] = scatter_rows(ray_hot[...], y[...])
+            if step == 0:
+                pl.semaphore_wait(barrier, count - 1)
+            picked[...] = gather_rows(ray_turned[...], exchange(step))
+            block_sweep(blocks_hbm, held, sems, picked, y, slices, False, False)
+            x[...] = x[...] - 0.8 * scatter_rows(tile_hot[...], y[...])
+
+        for z in range(slices):
+            for t in range(detectors):
+                moved = x[t * local:(t + 1) * local, z * LANES:(z + 1) * LANES]
+                at = slice(t * LANES, (t + 1) * LANES)
+                out_ref[z, :, at] = 2.0 * moved - cur[z, :, at]
+
+
+def data_reflect(angle, detector, tile, sinogram, current, blocks, count):
+    slices, local, columns = current.shape
+    rays_here = sinogram.shape[0]
+    ray_total = rays_here * count
+    tiles_here = columns // LANES * local
+    blocks_here = blocks.shape[0]
+    width = slices * LANES
+    vmem = pl.BlockSpec(memory_space=pltpu.VMEM)
+    anywhere = pl.BlockSpec(memory_space=pl.ANY)
     return pl.pallas_call(
-        functools.partial(ray_kernel, count),
-        out_shape=jax.ShapeDtypeStruct((count, rows, LANES), jnp.bfloat16),
-        in_specs=[whole] * 2,
-        out_specs=whole,
+        functools.partial(data_kernel, count),
+        out_shape=jax.ShapeDtypeStruct(current.shape, F32),
+        in_specs=[vmem] * 4 + [anywhere] * 2,
+        out_specs=vmem,
         scratch_shapes=[
-            pltpu.VMEM((count, rows, LANES), jnp.bfloat16),
-            pltpu.VMEM((rows, LANES), jnp.bfloat16),
-            pltpu.SemaphoreType.DMA((count,)),
-            pltpu.SemaphoreType.DMA((count,)),
-            pltpu.SemaphoreType.DMA((count,)),
-            pltpu.SemaphoreType.DMA((count,)),
+            pltpu.VMEM(blocks.shape, BF),
+            pltpu.VMEM(current.shape, F32),
+            pltpu.VMEM((ray_total, blocks_here), BF),
+            pltpu.VMEM((blocks_here, ray_total), BF),
+            pltpu.VMEM((tiles_here, blocks_here), BF),
+            pltpu.VMEM((blocks_here, tiles_here), BF),
+            pltpu.VMEM((tiles_here, width), F32),
+            pltpu.VMEM((blocks_here, width), F32),
+            pltpu.VMEM((blocks_here, width), F32),
+            pltpu.VMEM((ray_total, width), F32),
+            pltpu.VMEM((DATA_STEPS, count, rays_here, width), BF),
+            pltpu.VMEM((DATA_STEPS, count, rays_here, width), BF),
+            pltpu.VMEM((DATA_STEPS, rays_here, width), BF),
+            pltpu.VMEM((DATA_STEPS, count, rays_here, width), BF),
+            pltpu.SemaphoreType.DMA((1,)),
+            pltpu.SemaphoreType.DMA((blocks_here // CHUNK,)),
+            pltpu.SemaphoreType.DMA((DATA_STEPS, count)),
+            pltpu.SemaphoreType.DMA((DATA_STEPS, count)),
+            pltpu.SemaphoreType.DMA((DATA_STEPS, count)),
+            pltpu.SemaphoreType.DMA((DATA_STEPS, count)),
         ],
-        compiler_params=pltpu.CompilerParams(collective_id=0, has_side_effects=True),
-        name="ray_exchange",
-    )(part, sinogram)
-
-
-def agent_kernel(own_ref, out_ref, near, pair, far, send, recv):
+        compiler_params=pltpu.CompilerParams(
+            collective_id=0, has_side_effects=True, vmem_limit_bytes=40 * 1024 * 1024
+        ),
+        name="data_agent",
+    )(
+        angle.reshape(1, -1), detector.reshape(1, -1), tile.reshape(1, -1),
+        sinogram.reshape(rays_here * slices, LANES), current, blocks,
+    )
+
+
+def agent_kernel(own_ref, out_ref, own, near, pair, far, s1, r1, s2, r2, s3, r3, s4, r4):
     me = lax.axis_index("agent")
     tile = lax.axis_index("tile")
-    partner = me + 1 - 2 * (me % 2)
+    core = me % 2
+    other = 1 - core
+    partner = me + 1 - 2 * core
     across = (me + 2) % 4
+    chunks = pair.shape[0]
     barrier = pltpu.get_barrier_semaphore()
     for peer in (partner, across):
         pl.semaphore_signal(barrier, inc=1, device_id=(peer, tile), device_id_type=MESH)
+    own[...] = own_ref[...].astype(BF)
     pl.semaphore_wait(barrier, 2)
 
-    first = pltpu.make_async_remote_copy(
-        src_ref=own_ref,
-        dst_ref=near,
-        send_sem=send.at[0],
-        recv_sem=recv.at[0],
-        device_id=(partner, tile),
-        device_id_type=MESH,
-    )
-    first.start()
-    first.wait()
-    pair[...] = (own_ref[...].astype(jnp.float32) + near[...].astype(jnp.float32)).astype(jnp.bfloat16)
-    second = pltpu.make_async_remote_copy(
-        src_ref=pair,
-        dst_ref=far,
-        send_sem=send.at[1],
-        recv_sem=recv.at[1],
-        device_id=(across, tile),
-        device_id_type=MESH,
-    )
-    second.start()
-    second.wait()
-    out_ref[...] = near[...].astype(jnp.float32) + far[...].astype(jnp.float32)
-
-
-def agent_sum(own):
+    def send(source, target, s, r, to):
+        return pltpu.make_async_remote_copy(
+            src_ref=source, dst_ref=target, send_sem=s, recv_sem=r, device_id=(to, tile), device_id_type=MESH
+        )
+
+    def first(k, half):
+        return send(own.at[half, k], near.at[half, k], s1.at[k], r1.at[k], partner)
+
+    def rest(half):
+        return send(own.at[half], near.at[half], s2.at[0], r2.at[0], partner)
+
+    def cross(k):
+        return send(pair.at[k], far.at[core, k], s3.at[k], r3.at[k], across)
+
+    def onward(k, half):
+        return send(far.at[half, k], far.at[half, k], s4.at[k], r4.at[k], partner)
+
+    def result(half, k):
+        out_ref[half, k] = near[half, k].astype(F32) + far[half, k].astype(F32) - own_ref[half, k]
+
+    for k in range(chunks):
+        first(k, other).start()
+    rest(core).start()
+    for k in range(chunks):
+        first(k, core).wait_recv()
+        pair[k] = (own[core, k].astype(F32) + near[core, k].astype(F32)).astype(BF)
+        cross(k).start()
+    for k in range(chunks):
+        cross(k).wait_recv()
+        onward(k, core).start()
+        result(core, k)
+    rest(other).wait_recv()
+    for k in range(chunks):
+        onward(k, other).wait_recv()
+        result(other, k)
+    for k in range(chunks):
+        first(k, other).wait_send()
+        cross(k).wait_send()
+        onward(k, core).wait_send()
+    rest(core).wait_send()
+
+
+def agent_sum(reflect):
+    slices, local, columns = reflect.shape
+    half = slices * local // 2
+    chunks = max(1, half // 32)
+    shape = (2, chunks, half // chunks, columns)
     whole = pl.BlockSpec(memory_space=pltpu.VMEM)
-    return pl.pallas_call(
+    out = pl.pallas_call(
         agent_kernel,
-        out_shape=jax.ShapeDtypeStruct(own.shape, jnp.float32),
+        out_shape=jax.ShapeDtypeStruct(shape, F32),
         in_specs=[whole],
         out_specs=whole,
         scratch_shapes=[
-            pltpu.VMEM(own.shape, jnp.bfloat16),
-            pltpu.VMEM(own.shape, jnp.bfloat16),
-            pltpu.VMEM(own.shape, jnp.bfloat16),
-            pltpu.SemaphoreType.DMA((2,)),
-            pltpu.SemaphoreType.DMA((2,)),
+            pltpu.VMEM(shape, BF),
+            pltpu.VMEM(shape, BF),
+            pltpu.VMEM(shape[1:], BF),
+            pltpu.VMEM(shape, BF),
+            pltpu.SemaphoreType.DMA((chunks,)),
+            pltpu.SemaphoreType.DMA((chunks,)),
+            pltpu.SemaphoreType.DMA((1,)),
+            pltpu.SemaphoreType.DMA((1,)),
+            pltpu.SemaphoreType.DMA((chunks,)),
+            pltpu.SemaphoreType.DMA((chunks,)),
+            pltpu.SemaphoreType.DMA((chunks,)),
+            pltpu.SemaphoreType.DMA((chunks,)),
         ],
         compiler_params=pltpu.CompilerParams(collective_id=1, has_side_effects=True),
         name="agent_sum",
-    )(own)
+    )(reflect.reshape(shape))
+    return out.reshape(reflect.shape)
 
 
 def per_device(
@@ -808,72 +834,28 @@
     conv_last,
 ):
     current = states[0]
-    slices, local_rows, image_columns = current.shape
-    tile_count = lax.axis_size("tile")
     agent_place = lax.axis_index("agent")
-    is_data = agent_place == 0
-    tiles_here = local_rows * image_columns // LANES
-    rays_here = sinogram.shape[0]
-    ray_total = rays_here * tile_count
-    part_shape = (tile_count, rays_here * slices, LANES)
     halo = conv_hidden.shape[1] + 2
     filters = (conv_first, conv_hidden, conv_last)
-    rays = block_angle * (image_columns // LANES) + block_detector
-    pixel_shape = jax.ShapeDtypeStruct((tiles_here, 2 * slices, LANES), F32)
-    part_type = jax.ShapeDtypeStruct((ray_total * slices, LANES), BF)
-    ray_shape = (ray_total, 2 * slices, LANES)
-
-    def tiled():
-        pixels = jnp.transpose(current.reshape(slices, tiles_here, LANES), (1, 0, 2))
-        return jnp.concatenate([pixels, pixels], axis=1)
-
     edges = halo_exchange(current, halo)
-    no_part = jnp.zeros(part_shape, BF)
-    no_pixels = jnp.zeros(pixel_shape.shape, F32)
-
-    def data_start():
-        pixels = tiled()
-        part = data_call(project_kernel, "project", (rays, block_tile, blocks, pixels), part_type, blocks, [ray_shape])
-        return part.reshape(part_shape), pixels, current
+    data = data_reflect(
+        block_angle, block_detector, block_tile, sinogram, current, blocks, lax.axis_size("tile")
+    )
+
+    def data_only():
+        return data
 
     def axial_only():
-        return no_part, no_pixels, axial_reflect(edges, current, *filters, halo)
+        return axial_reflect(edges, current, *filters, halo)
 
     def sagittal_only():
-        return no_part, no_pixels, plane_call(1, edges, current, *filters, halo, 1)
+        return plane_call(1, edges, current, *filters, halo, 1)
 
     def coronal_only():
-        return no_part, no_pixels, coronal_reflect(current, *filters)
-
-    part, pixels, reflect = lax.switch(agent_place, [data_start, axial_only, sagittal_only, coronal_only])
-    own_sinogram = sinogram.reshape(rays_here * slices, LANES)
-    first = pixels
-
-    for step in range(DATA_STEPS):
-        residual = ray_exchange(part, own_sinogram, tile_count)
-        if step < DATA_STEPS - 1:
-
-            def advance(pixels, residual):
-                ins = (rays, block_tile, blocks, residual.reshape(part_type.shape), pixels)
-                part, moved = data_call(
-                    advance_kernel, "advance", ins, (part_type, pixel_shape), blocks, [ray_shape, ray_shape]
-                )
-                return part.reshape(part_shape), moved
-
-            part, pixels = lax.cond(is_data, advance, lambda p, r: (no_part, p), pixels, residual)
-        else:
-
-            def settle(pixels, first, reflect, residual):
-                ins = (rays, block_tile, blocks, residual.reshape(part_type.shape), pixels, first)
-                out = data_call(settle_kernel, "settle", ins, pixel_shape, blocks, [ray_shape])
-                return jnp.transpose(out[:, :slices], (1, 0, 2)).reshape(reflect.shape)
-
-            reflect = lax.cond(is_data, settle, lambda p, f, s, r: s, pixels, first, reflect, residual)
-
-    sent = reflect.astype(BF).reshape(slices * local_rows, image_columns)
-    others = agent_sum(sent).reshape(reflect.shape)
-    new_states = 0.5 * current + 0.25 * others - 0.25 * reflect
-    return new_states[None]
+        return coronal_reflect(current, *filters)
+
+    reflect = lax.switch(agent_place, [data_only, axial_only, sagittal_only, coronal_only])
+    return (0.5 * current + 0.25 * agent_sum(reflect))[None]
 
 
 def solution(mesh):

time: 68.5 us -> 57.5 us (0.84)
  Pallas kernels: 62.2 us -> 48.6 us
  local copies, waits for them, and re-layouts: 1.79 us -> 6.26 us
  other arithmetic: 3.65 us -> 1.97 us
    pallas_call x6 -> x2, Pallas kernels: 62.2 us -> 48.5 us  [the longest x1 40.5 us: data_reflect(): pl.pallas_call(functools.partial(data_kernel, count), out_shape=jax.Shape...]
    unnamed x2 -> x12, local copies, waits for them, and re-layouts: 0.01 us -> 6.26 us
    another operation x2 -> x0, local copies, waits for them, and re-layouts: 1.42 us -> none  [tiled(): current.reshape(slices, tiles_here, LANES)]
    broadcast_in_dim x1 -> x0, other arithmetic: 0.96 us -> none  [per_device(): return new_states[None]]
    convert_element_type x1 -> x0, other arithmetic: 0.74 us -> none  [per_device(): sent = reflect.astype(BF).reshape(slices * local_rows, image_columns)]
where the time goes in v2:
time: 57.5 us; the launch traced here: 57.1 us
  Pallas kernels  48.6 us (85%)
  local copies, waits for them, and re-layouts  6.26 us (11%)
  other arithmetic  1.97 us (3%)
    pallas_call x1, Pallas kernels, data_reflect(): pl.pallas_call(functools.partial(data_kernel, count), out_shape=jax.Shape...  40.5 us
    pallas_call x1, Pallas kernels, agent_sum(): pl.pallas_call(agent_kernel, out_shape=jax.ShapeDtypeStruct(shape, F32),...  8.01 us
    unnamed x12, local copies, waits for them, and re-layouts  6.26 us

profile of v2, /device:TPU:0, one launch (start us, length us, event | category | flops | bytes accessed | tf_op | source)
XLA Modules:
  0.0 57.1 jit_solution(5213652822332694067)
XLA Ops:
  0.0 0.1 halo_exchange.1
  0.1 0.0 copy-start
  0.1 3.4 %copy-done = bf16[256,128,128]{2,1,0:T(8,128)(2,1)S(1)} copy-done((bf16[256,128,128]{2,1,0:T(8,128)(2,1)S(1)}, bf16[256,128,128]{2,1,0:T(8,128)(2,1)}, u32[]{:S(2)}) %copy-start) | copy-done | bytes 8388632
  3.4 0.0 copy-start.1
  3.4 0.8 %copy-done.1 = f32[32,4,128]{2,1,0:T(4,128)S(1)} copy-done((f32[32,4,128]{2,1,0:T(4,128)S(1)}, f32[32,4,128]{2,1,0:T(4,128)}, u32[]{:S(2)}) %copy-start.1) | copy-done | bytes 65560
  4.3 0.0 copy-start.2
  4.3 0.7 %copy-done.2 = s32[256]{0:T(256)S(1)} copy-done((s32[256]{0:T(256)S(1)}, s32[256]{0:T(256)}, u32[]{:S(2)}) %copy-start.2) | copy-done | bytes 1048
  5.0 0.0 copy-start.3
  5.0 0.7 %copy-done.3 = s32[256]{0:T(256)S(1)} copy-done((s32[256]{0:T(256)S(1)}, s32[256]{0:T(256)}, u32[]{:S(2)}) %copy-start.3) | copy-done | bytes 1048
  5.6 0.0 copy-start.4
  5.6 0.7 %copy-done.4 = s32[256]{0:T(256)S(1)} copy-done((s32[256]{0:T(256)S(1)}, s32[256]{0:T(256)}, u32[]{:S(2)}) %copy-start.4) | copy-done | bytes 1048
  6.3 40.5 %data_agent.1 = f32[4,64,512]{2,1,0:T(8,128)S(1)} custom-call(s32[1,256]{1,0:T(1,128)S(1)} %bitcast.19, s32[1,256]{1,0:T(1,128)S(1)} %bitcast.20, s32[1,256]{1,0:T(1,128)S(1)} %bitcast.21, f32[128,128]{1,0:T(8,128)S(1)} %bitcast.18, f32[4,64,512]{2,1,0:T(8,128)} %bitcast.23, bf16[256,128,128]{2,1,0:T(8,128)(2,1)S(1)} %copy-done), custom_call_target="tpu_custom_call" | custom-call | tf_op jit(solution)/shard_map/data_agent/pallas_call | solution.py:701
  46.8 0.2 conditional.1
  47.1 0.0 copy-start.5
  47.1 8.0 %agent_sum.1 = f32[2,4,32,512]{3,2,1,0:T(8,128)} custom-call(f32[2,4,32,512]{3,2,1,0:T(8,128)S(1)} %bitcast.28), custom_call_target="tpu_custom_call" | custom-call | tf_op jit(solution)/shard_map/agent_sum/pallas_call | solution.py:800
  55.1 1.1 %broadcast_multiply_fusion = f32[2,4,32,512]{3,2,1,0:T(8,128)S(1)} fusion(f32[2,4,32,512]{3,2,1,0:T(8,128)} %agent_sum.1), kind=kLoop, calls=%fused_computation.11 | loop fusion | flops 131072 | bytes 1048576 | tf_op jit(solution)/shard_map/mul | solution.py:858
  56.2 0.0 copy-done.5
  56.2 0.9 %multiply_add_fusion = f32[1,4,64,512]{3,2,1,0:T(8,128)} fusion(f32[1,4,64,512]{3,2,1,0:T(8,128)S(1)} %bitcast.29, f32[1,4,64,512]{3,2,1,0:T(8,128)S(1)} %copy-done.5), kind=kLoop, calls=%fused_computation.10 | loop fusion | flops 262144 | bytes 1572864 | tf_op jit(solution)/shard_map/add | solution.py:858
Async XLA Ops:
  0.1 3.4 %copy-start = (bf16[256,128,128]{2,1,0:T(8,128)(2,1)S(1)}, bf16[256,128,128]{2,1,0:T(8,128)(2,1)}, u32[]{:S(2)}) copy-start(bf16[256,128,128]{2,1,0:T(8,128)(2,1)} %blocks_hbm.1) | copy-start | bytes 25165828
  3.4 0.8 %copy-start.1 = (f32[32,4,128]{2,1,0:T(4,128)S(1)}, f32[32,4,128]{2,1,0:T(4,128)}, u32[]{:S(2)}) copy-start(f32[32,4,128]{2,1,0:T(4,128)} %param.14) | copy-start | bytes 196612
  4.3 0.7 %copy-start.2 = (s32[256]{0:T(256)S(1)}, s32[256]{0:T(256)}, u32[]{:S(2)}) copy-start(s32[256]{0:T(256)} %param.16) | copy-start | bytes 3076
  5.0 0.7 %copy-start.3 = (s32[256]{0:T(256)S(1)}, s32[256]{0:T(256)}, u32[]{:S(2)}) copy-start(s32[256]{0:T(256)} %param.17) | copy-start | bytes 3076
  5.6 0.7 %copy-start.4 = (s32[256]{0:T(256)S(1)}, s32[256]{0:T(256)}, u32[]{:S(2)}) copy-start(s32[256]{0:T(256)} %param.18) | copy-start | bytes 3076
  47.1 9.1 %copy-start.5 = (f32[1,4,64,512]{3,2,1,0:T(8,128)S(1)}, f32[1,4,64,512]{3,2,1,0:T(8,128)}, u32[]{:S(2)}) copy-start(f32[1,4,64,512]{3,2,1,0:T(8,128)} %param.13) | copy-start | bytes 1572868

commit v3 on v2

--- a/solution.py
+++ b/solution.py
@@ -726,7 +726,7 @@
             pltpu.SemaphoreType.DMA((DATA_STEPS, count)),
         ],
         compiler_params=pltpu.CompilerParams(
-            collective_id=0, has_side_effects=True, vmem_limit_bytes=40 * 1024 * 1024
+            collective_id=0, has_side_effects=True, vmem_limit_bytes=62 * 1024 * 1024
         ),
         name="data_agent",
     )(
@@ -735,7 +735,7 @@
     )
 
 
-def agent_kernel(own_ref, out_ref, own, near, pair, far, s1, r1, s2, r2, s3, r3, s4, r4):
+def agent_kernel(own_ref, cur_hbm, out_ref, cur, own, near, pair, far, load, s1, r1, s2, r2, s3, r3, s4, r4):
     me = lax.axis_index("agent")
     tile = lax.axis_index("tile")
     core = me % 2
@@ -746,6 +746,8 @@
     barrier = pltpu.get_barrier_semaphore()
     for peer in (partner, across):
         pl.semaphore_signal(barrier, inc=1, device_id=(peer, tile), device_id_type=MESH)
+    state = pltpu.make_async_copy(cur_hbm, cur, load.at[0])
+    state.start()
     own[...] = own_ref[...].astype(BF)
     pl.semaphore_wait(barrier, 2)
 
@@ -767,7 +769,8 @@
         return send(far.at[half, k], far.at[half, k], s4.at[k], r4.at[k], partner)
 
     def result(half, k):
-        out_ref[half, k] = near[half, k].astype(F32) + far[half, k].astype(F32) - own_ref[half, k]
+        others = near[half, k].astype(F32) + far[half, k].astype(F32)
+        out_ref[half, k] = 2.0 * cur[half, k] + others - own_ref[half, k]
 
     for k in range(chunks):
         first(k, other).start()
@@ -776,6 +779,7 @@
         first(k, core).wait_recv()
         pair[k] = (own[core, k].astype(F32) + near[core, k].astype(F32)).astype(BF)
         cross(k).start()
+    state.wait()
     for k in range(chunks):
         cross(k).wait_recv()
         onward(k, core).start()
@@ -791,7 +795,7 @@
     rest(core).wait_send()
 
 
-def agent_sum(reflect):
+def agent_sum(reflect, current):
     slices, local, columns = reflect.shape
     half = slices * local // 2
     chunks = max(1, half // 32)
@@ -800,13 +804,15 @@
     out = pl.pallas_call(
         agent_kernel,
         out_shape=jax.ShapeDtypeStruct(shape, F32),
-        in_specs=[whole],
+        in_specs=[whole, pl.BlockSpec(memory_space=pl.ANY)],
         out_specs=whole,
         scratch_shapes=[
+            pltpu.VMEM(shape, F32),
             pltpu.VMEM(shape, BF),
             pltpu.VMEM(shape, BF),
             pltpu.VMEM(shape[1:], BF),
             pltpu.VMEM(shape, BF),
+            pltpu.SemaphoreType.DMA((1,)),
             pltpu.SemaphoreType.DMA((chunks,)),
             pltpu.SemaphoreType.DMA((chunks,)),
             pltpu.SemaphoreType.DMA((1,)),
@@ -818,7 +824,7 @@
         ],
         compiler_params=pltpu.CompilerParams(collective_id=1, has_side_effects=True),
         name="agent_sum",
-    )(reflect.reshape(shape))
+    )(reflect.reshape(shape), current.reshape(shape))
     return out.reshape(reflect.shape)
 
 
@@ -855,7 +861,7 @@
         return coronal_reflect(current, *filters)
 
     reflect = lax.switch(agent_place, [data_only, axial_only, sagittal_only, coronal_only])
-    return (0.5 * current + 0.25 * agent_sum(reflect))[None]
+    return (0.25 * agent_sum(reflect, current))[None]
 
 
 def solution(mesh):

time: 57.5 us -> 54.1 us (0.941)
  local copies, waits for them, and re-layouts: 6.26 us -> 0 us
  Pallas kernels: 48.6 us -> 51.7 us
    unnamed x12 -> x0, local copies, waits for them, and re-layouts: 6.26 us -> none
    pallas_call x1, Pallas kernels: 40.5 us -> 43.6 us  [data_reflect(): pl.pallas_call(functools.partial(data_kernel, count), out_shape=jax.Shape...]
    add x1 -> x0, other arithmetic: 0.88 us -> none  [per_device(): return (0.5 * current + 0.25 * agent_sum(reflect))[None]]
    mul x1, other arithmetic: 1.08 us -> 1.88 us  [per_device(): return (0.25 * agent_sum(reflect, current))[None]]
where the time goes in v3:
time: 54.1 us; the launch traced here: 53.8 us
  Pallas kernels  51.7 us (96%)
  other arithmetic  1.88 us (3%)
    pallas_call x1, Pallas kernels, data_reflect(): pl.pallas_call(functools.partial(data_kernel, count), out_shape=jax.Shape...  43.6 us
    pallas_call x1, Pallas kernels, agent_sum(): pl.pallas_call(agent_kernel, out_shape=jax.ShapeDtypeStruct(shape, F32),...  8.02 us
    mul x1, other arithmetic, per_device(): return (0.25 * agent_sum(reflect, current))[None]  1.88 us

profile of v3, /device:TPU:0, one launch (start us, length us, event | category | flops | bytes accessed | tf_op | source)
XLA Modules:
  0.0 53.8 jit_solution(13128835691166023394)
XLA Ops:
  0.0 0.1 halo_exchange.1
  0.1 43.6 %data_agent.1 = f32[4,64,512]{2,1,0:T(8,128)S(1)} custom-call(s32[1,256]{1,0:T(1,128)} %bitcast.32, s32[1,256]{1,0:T(1,128)} %bitcast.33, s32[1,256]{1,0:T(1,128)} %bitcast.34, f32[128,128]{1,0:T(8,128)} %bitcast.31, f32[4,64,512]{2,1,0:T(8,128)} %bitcast.22, bf16[256,128,128]{2,1,0:T(8,128)(2,1)} %blocks_hbm.1), custom_call_target="tpu_custom_call" | custom-call | tf_op jit(solution)/shard_map/data_agent/pallas_call | solution.py:701
  43.7 0.2 conditional.1
  43.9 8.0 %agent_sum.1 = f32[2,4,32,512]{3,2,1,0:T(8,128)} custom-call(f32[2,4,32,512]{3,2,1,0:T(8,128)S(1)} %get-tuple-element.57.own_ref, f32[2,4,32,512]{3,2,1,0:T(8,128)} %bitcast.25), custom_call_target="tpu_custom_call" | custom-call | tf_op jit(solution)/shard_map/agent_sum/pallas_call | solution.py:804
  51.9 1.9 %broadcast_multiply_fusion = f32[2,4,32,512]{3,2,1,0:T(8,128)} fusion(f32[2,4,32,512]{3,2,1,0:T(8,128)} %agent_sum.1), kind=kLoop, calls=%fused_computation.10 | loop fusion | flops 131072 | bytes 1048576 | tf_op jit(solution)/shard_map/mul | solution.py:864

commit v4 on v2

--- a/solution.py
+++ b/solution.py
@@ -588,20 +588,47 @@
     )
 
 
-def data_kernel(
-    count, angle_ref, detector_ref, tile_ref, sino_ref, cur_hbm, blocks_hbm, out_ref,
+def join_kernel(
+    plan, angle_ref, detector_ref, tile_ref, sino_ref, reflect_ref, cur_hbm, blocks_hbm, out_ref,
     held, cur, ray_hot, ray_turned, tile_hot, tile_turned, x, y, picked, total, part, got, fresh, full,
-    load, sems, send1, recv1, send2, recv2,
+    own, pair, beside, across, onward,
+    load, sems, send1, recv1, send2, recv2, ready,
+    send_beside, recv_beside, send_across, recv_across, send_onward, recv_onward,
 ):
     agent = lax.axis_index("agent")
     me = lax.axis_index("tile")
-    slices, local, columns = out_ref.shape
+    count, slices = plan
+    chunks, height, columns = own.shape
+    local = chunks * height // slices
     detectors = columns // LANES
     rays_here = fresh.shape[1]
     ray_total = count * rays_here
     tiles_here = detectors * local
     blocks_here = held.shape[0]
     order = list(range(count - 1, 0, -1))
+    core = agent % 2
+    neighbour = agent + 1 - 2 * core
+    opposite = (agent + 2) % 4
+    state = pltpu.make_async_copy(cur_hbm, cur, load.at[0])
+    state.start()
+
+    def send(source, target, s, r, k, to):
+        return pltpu.make_async_remote_copy(
+            src_ref=source.at[k], dst_ref=target.at[k], send_sem=s.at[k], recv_sem=r.at[k],
+            device_id=(to, me), device_id_type=MESH,
+        )
+
+    def to_beside(k):
+        return send(own, beside, send_beside, recv_beside, k, neighbour)
+
+    def to_across(source, k):
+        return send(source, across, send_across, recv_across, k, opposite)
+
+    def to_onward(k):
+        return send(across, onward, send_onward, recv_onward, k, neighbour)
+
+    def rows_of(k):
+        return slice(k * height, (k + 1) * height)
 
     def part_copy(step, d):
         return pltpu.make_async_remote_copy(
@@ -650,8 +677,8 @@
         barrier = pltpu.get_barrier_semaphore()
         for d in order:
             pl.semaphore_signal(barrier, inc=1, device_id=(agent, swap_bits(me, d)), device_id_type=MESH)
-        first = pltpu.make_async_copy(cur_hbm, cur, load.at[0])
-        first.start()
+        for peer in (neighbour, opposite):
+            pl.semaphore_signal(barrier, inc=1, device_id=(peer, me), device_id_type=MESH)
         for i in range(blocks_here // CHUNK):
             block_copy(blocks_hbm, held, sems, i).start()
 
@@ -667,10 +694,10 @@
         tile_hot[...] = hot.astype(BF)
         tile_turned[...] = hot.T.astype(BF)
 
-        first.wait()
+        state.wait()
         for z in range(slices):
             for t in range(detectors):
-                x[t * local:(t + 1) * local, z * LANES:(z + 1) * LANES] = cur[z, :, t * LANES:(t + 1) * LANES]
+                x[t * local:(t + 1) * local, z * LANES:(z + 1) * LANES] = cur[z * local:(z + 1) * local, t * LANES:(t + 1) * LANES]
 
         for step in range(DATA_STEPS):
             picked[...] = gather_rows(tile_turned[...], x[...].astype(BF))
@@ -685,27 +712,96 @@
         for z in range(slices):
             for t in range(detectors):
                 moved = x[t * local:(t + 1) * local, z * LANES:(z + 1) * LANES]
-                at = slice(t * LANES, (t + 1) * LANES)
-                out_ref[z, :, at] = 2.0 * moved - cur[z, :, at]
-
-
-def data_reflect(angle, detector, tile, sinogram, current, blocks, count):
+                at = (slice(z * local, (z + 1) * local), slice(t * LANES, (t + 1) * LANES))
+                out_ref[at] = 2.0 * moved - cur[at]
+        for k in range(chunks):
+            own[k] = out_ref[rows_of(k), :].astype(BF)
+        out_ref[...] = 2.0 * cur[...] - out_ref[...]
+        pl.semaphore_wait(ready.at[0], 2)
+
+    @pl.when(agent != 0)
+    def _():
+        barrier = pltpu.get_barrier_semaphore()
+
+        @pl.when(agent != 1)
+        def _():
+            pl.semaphore_signal(barrier, inc=1, device_id=(neighbour, me), device_id_type=MESH)
+
+        @pl.when(agent != 2)
+        def _():
+            pl.semaphore_signal(barrier, inc=1, device_id=(opposite, me), device_id_type=MESH)
+
+        for k in range(chunks):
+            own[k] = reflect_ref[rows_of(k), :].astype(BF)
+        state.wait()
+        out_ref[...] = 2.0 * cur[...] - reflect_ref[...]
+        pl.semaphore_wait(barrier, 2)
+
+        @pl.when(agent != 3)
+        def _():
+            pl.semaphore_signal(ready.at[0], inc=1, device_id=(0, me), device_id_type=MESH)
+
+    def add(k, others):
+        out_ref[rows_of(k), :] = out_ref[rows_of(k), :] + others
+
+    @pl.when(agent < 2)
+    def _():
+        for k in range(chunks):
+            to_across(own, k).start()
+            to_beside(k).start()
+        for k in range(chunks):
+            to_beside(k).wait_recv()
+            to_across(own, k).wait_recv()
+            add(k, beside[k].astype(F32) + across[k].astype(F32))
+        for k in range(chunks):
+            to_across(own, k).wait_send()
+            to_beside(k).wait_send()
+
+    @pl.when(agent >= 2)
+    def _():
+        for k in range(chunks):
+            to_beside(k).start()
+        for k in range(chunks):
+            to_beside(k).wait_recv()
+            pair[k] = (own[k].astype(F32) + beside[k].astype(F32)).astype(BF)
+            to_across(pair, k).start()
+        for k in range(chunks):
+            to_across(pair, k).wait_recv()
+            to_onward(k).start()
+            add(k, beside[k].astype(F32) + across[k].astype(F32))
+        for k in range(chunks):
+            to_onward(k).wait_recv()
+            add(k, onward[k].astype(F32))
+        for k in range(chunks):
+            to_beside(k).wait_send()
+            to_across(pair, k).wait_send()
+            to_onward(k).wait_send()
+
+
+def idle_kernel(out_ref):
+    pass
+
+
+def join(angle, detector, tile, sinogram, reflect, current, blocks, count):
     slices, local, columns = current.shape
     rays_here = sinogram.shape[0]
     ray_total = rays_here * count
     tiles_here = columns // LANES * local
     blocks_here = blocks.shape[0]
     width = slices * LANES
+    rows = slices * local
+    chunks = max(1, rows // 32)
+    chunk = (chunks, rows // chunks, columns)
     vmem = pl.BlockSpec(memory_space=pltpu.VMEM)
     anywhere = pl.BlockSpec(memory_space=pl.ANY)
-    return pl.pallas_call(
-        functools.partial(data_kernel, count),
-        out_shape=jax.ShapeDtypeStruct(current.shape, F32),
-        in_specs=[vmem] * 4 + [anywhere] * 2,
+    out = pl.pallas_call(
+        functools.partial(join_kernel, (count, slices)),
+        out_shape=jax.ShapeDtypeStruct((rows, columns), F32),
+        in_specs=[vmem] * 5 + [anywhere] * 2,
         out_specs=vmem,
         scratch_shapes=[
             pltpu.VMEM(blocks.shape, BF),
-            pltpu.VMEM(current.shape, F32),
+            pltpu.VMEM((rows, columns), F32),
             pltpu.VMEM((ray_total, blocks_here), BF),
             pltpu.VMEM((blocks_here, ray_total), BF),
             pltpu.VMEM((tiles_here, blocks_here), BF),
@@ -718,108 +814,22 @@
             pltpu.VMEM((DATA_STEPS, count, rays_here, width), BF),
             pltpu.VMEM((DATA_STEPS, rays_here, width), BF),
             pltpu.VMEM((DATA_STEPS, count, rays_here, width), BF),
-            pltpu.SemaphoreType.DMA((1,)),
-            pltpu.SemaphoreType.DMA((blocks_here // CHUNK,)),
-            pltpu.SemaphoreType.DMA((DATA_STEPS, count)),
-            pltpu.SemaphoreType.DMA((DATA_STEPS, count)),
-            pltpu.SemaphoreType.DMA((DATA_STEPS, count)),
-            pltpu.SemaphoreType.DMA((DATA_STEPS, count)),
-        ],
+        ]
+        + [pltpu.VMEM(chunk, BF)] * 5
+        + [pltpu.SemaphoreType.DMA((1,)), pltpu.SemaphoreType.DMA((blocks_here // CHUNK,))]
+        + [pltpu.SemaphoreType.DMA((DATA_STEPS, count))] * 4
+        + [pltpu.SemaphoreType.REGULAR((1,))]
+        + [pltpu.SemaphoreType.DMA((chunks,))] * 6,
         compiler_params=pltpu.CompilerParams(
-            collective_id=0, has_side_effects=True, vmem_limit_bytes=40 * 1024 * 1024
+            collective_id=0, has_side_effects=True, vmem_limit_bytes=58 * 1024 * 1024
         ),
-        name="data_agent",
+        name="join_agents",
     )(
         angle.reshape(1, -1), detector.reshape(1, -1), tile.reshape(1, -1),
-        sinogram.reshape(rays_here * slices, LANES), current, blocks,
+        sinogram.reshape(rays_here * slices, LANES), reflect.reshape(rows, columns),
+        current.reshape(rows, columns), blocks,
     )
-
-
-def agent_kernel(own_ref, out_ref, own, near, pair, far, s1, r1, s2, r2, s3, r3, s4, r4):
-    me = lax.axis_index("agent")
-    tile = lax.axis_index("tile")
-    core = me % 2
-    other = 1 - core
-    partner = me + 1 - 2 * core
-    across = (me + 2) % 4
-    chunks = pair.shape[0]
-    barrier = pltpu.get_barrier_semaphore()
-    for peer in (partner, across):
-        pl.semaphore_signal(barrier, inc=1, device_id=(peer, tile), device_id_type=MESH)
-    own[...] = own_ref[...].astype(BF)
-    pl.semaphore_wait(barrier, 2)
-
-    def send(source, target, s, r, to):
-        return pltpu.make_async_remote_copy(
-            src_ref=source, dst_ref=target, send_sem=s, recv_sem=r, device_id=(to, tile), device_id_type=MESH
-        )
-
-    def first(k, half):
-        return send(own.at[half, k], near.at[half, k], s1.at[k], r1.at[k], partner)
-
-    def rest(half):
-        return send(own.at[half], near.at[half], s2.at[0], r2.at[0], partner)
-
-    def cross(k):
-        return send(pair.at[k], far.at[core, k], s3.at[k], r3.at[k], across)
-
-    def onward(k, half):
-        return send(far.at[half, k], far.at[half, k], s4.at[k], r4.at[k], partner)
-
-    def result(half, k):
-        out_ref[half, k] = near[half, k].astype(F32) + far[half, k].astype(F32) - own_ref[half, k]
-
-    for k in range(chunks):
-        first(k, other).start()
-    rest(core).start()
-    for k in range(chunks):
-        first(k, core).wait_recv()
-        pair[k] = (own[core, k].astype(F32) + near[core, k].astype(F32)).astype(BF)
-        cross(k).start()
-    for k in range(chunks):
-        cross(k).wait_recv()
-        onward(k, core).start()
-        result(core, k)
-    rest(other).wait_recv()
-    for k in range(chunks):
-        onward(k, other).wait_recv()
-        result(other, k)
-    for k in range(chunks):
-        first(k, other).wait_send()
-        cross(k).wait_send()
-        onward(k, core).wait_send()
-    rest(core).wait_send()
-
-
-def agent_sum(reflect):
-    slices, local, columns = reflect.shape
-    half = slices * local // 2
-    chunks = max(1, half // 32)
-    shape = (2, chunks, half // chunks, columns)
-    whole = pl.BlockSpec(memory_space=pltpu.VMEM)
-    out = pl.pallas_call(
-        agent_kernel,
-        out_shape=jax.ShapeDtypeStruct(shape, F32),
-        in_specs=[whole],
-        out_specs=whole,
-        scratch_shapes=[
-            pltpu.VMEM(shape, BF),
-            pltpu.VMEM(shape, BF),
-            pltpu.VMEM(shape[1:], BF),
-            pltpu.VMEM(shape, BF),
-            pltpu.SemaphoreType.DMA((chunks,)),
-            pltpu.SemaphoreType.DMA((chunks,)),
-            pltpu.SemaphoreType.DMA((1,)),
-            pltpu.SemaphoreType.DMA((1,)),
-            pltpu.SemaphoreType.DMA((chunks,)),
-            pltpu.SemaphoreType.DMA((chunks,)),
-            pltpu.SemaphoreType.DMA((chunks,)),
-            pltpu.SemaphoreType.DMA((chunks,)),
-        ],
-        compiler_params=pltpu.CompilerParams(collective_id=1, has_side_effects=True),
-        name="agent_sum",
-    )(reflect.reshape(shape))
-    return out.reshape(reflect.shape)
+    return out.reshape(current.shape)
 
 
 def per_device(
@@ -838,12 +848,14 @@
     halo = conv_hidden.shape[1] + 2
     filters = (conv_first, conv_hidden, conv_last)
     edges = halo_exchange(current, halo)
-    data = data_reflect(
-        block_angle, block_detector, block_tile, sinogram, current, blocks, lax.axis_size("tile")
-    )
 
     def data_only():
-        return data
+        return pl.pallas_call(
+            idle_kernel,
+            out_shape=jax.ShapeDtypeStruct(current.shape, F32),
+            out_specs=pl.BlockSpec(memory_space=pl.ANY),
+            name="idle",
+        )()
 
     def axial_only():
         return axial_reflect(edges, current, *filters, halo)
@@ -855,7 +867,10 @@
         return coronal_reflect(current, *filters)
 
     reflect = lax.switch(agent_place, [data_only, axial_only, sagittal_only, coronal_only])
-    return (0.5 * current + 0.25 * agent_sum(reflect))[None]
+    joined = join(
+        block_angle, block_detector, block_tile, sinogram, reflect, current, blocks, lax.axis_size("tile")
+    )
+    return (0.25 * joined)[None]
 
 
 def solution(mesh):

time: 57.5 us -> 51.2 us (0.89)
  local copies, waits for them, and re-layouts: 6.26 us -> 0 us
    unnamed x12 -> x0, local copies, waits for them, and re-layouts: 6.26 us -> none
    add x1 -> x0, other arithmetic: 0.88 us -> none  [per_device(): return (0.5 * current + 0.25 * agent_sum(reflect))[None]]
    mul x1, other arithmetic: 1.08 us -> 1.88 us  [per_device(): return (0.25 * joined)[None]]
where the time goes in v4:
time: 51.2 us; the launch traced here: 50.9 us
  Pallas kernels  48.7 us (95%)
  other arithmetic  1.88 us (4%)
    pallas_call x1, Pallas kernels, join(): pl.pallas_call(functools.partial(join_kernel, (count, slices)), out_shape...  48.7 us
    mul x1, other arithmetic, per_device(): return (0.25 * joined)[None]  1.88 us

profile of v4, /device:TPU:0, one launch (start us, length us, event | category | flops | bytes accessed | tf_op | source)
XLA Modules:
  0.0 50.9 jit_solution(3390480041444295738)
XLA Ops:
  0.0 0.1 halo_exchange.1
  0.1 0.2 conditional.1
  0.3 48.7 %join_agents.1 = f32[256,512]{1,0:T(8,128)} custom-call(s32[1,256]{1,0:T(1,128)} %bitcast.31, s32[1,256]{1,0:T(1,128)} %bitcast.32, s32[1,256]{1,0:T(1,128)} %bitcast.33, f32[128,128]{1,0:T(8,128)} %bitcast.30, f32[256,512]{1,0:T(8,128)S(1)} %get-tuple-element.55.reflect_ref, f32[256,512]{1,0:T(8,128)} %bitcast.24, bf16[256,128,128]{2,1,0:T(8,128)(2,1)} %blocks_hbm.1), custom_call_target="tpu_custom_call" | custom-call | tf_op jit(solution)/shard_map/join_agents/pallas_call | solution.py:797
  49.0 1.9 %broadcast_multiply_fusion = f32[256,512]{1,0:T(8,128)} fusion(f32[256,512]{1,0:T(8,128)} %join_agents.1), kind=kLoop, calls=%fused_computation.10 | loop fusion | flops 131072 | bytes 1048576 | tf_op jit(solution)/shard_map/mul | solution.py:873
  (1 shorter events, 0.0 us)

commit v5 on v4

--- a/solution.py
+++ b/solution.py
@@ -11,7 +11,8 @@
 MESH = pl.DeviceIdType.MESH
 LANES = 128
 STRIPS = 16
-CHUNK = 32
+CHUNK = 64
+SPAN = 256
 BF = jnp.bfloat16
 F32 = jnp.float32
 NATURAL = (0, 1, 2, 3)
@@ -566,14 +567,16 @@
 
 
 def block_sweep(blocks_hbm, held, sems, picked, y, slices, transposed, waiting):
+    span = min(SPAN, held.shape[0])
+
     def chunk(i, carry):
-        if waiting:
-            block_copy(blocks_hbm, held, sems, i).wait()
-        for j in range(CHUNK // 8):
-            block_step(held, picked, y, slices, transposed, i * (CHUNK // 8) + j)
+        for j in range(span // 8):
+            if waiting and j % (CHUNK // 8) == 0:
+                block_copy(blocks_hbm, held, sems, i * (span // CHUNK) + j // (CHUNK // 8)).wait()
+            block_step(held, picked, y, slices, transposed, i * (span // 8) + j)
         return carry
 
-    lax.fori_loop(0, held.shape[0] // CHUNK, chunk, 0)
+    lax.fori_loop(0, held.shape[0] // span, chunk, 0)
 
 
 def gather_rows(hot, source):
@@ -796,7 +799,7 @@
     anywhere = pl.BlockSpec(memory_space=pl.ANY)
     out = pl.pallas_call(
         functools.partial(join_kernel, (count, slices)),
-        out_shape=jax.ShapeDtypeStruct((rows, columns), F32),
+        out_shape=pltpu.VMEM((rows, columns), F32),
         in_specs=[vmem] * 5 + [anywhere] * 2,
         out_specs=vmem,
         scratch_shapes=[

time: 51.2 us -> 49.3 us (0.963)
  other arithmetic: 1.88 us -> 0.84 us
  Pallas kernels: 48.7 us -> 47.9 us
    mul x1, other arithmetic: 1.88 us -> 0.84 us  [per_device(): return (0.25 * joined)[None]]
    pallas_call x1, Pallas kernels: 48.7 us -> 47.9 us  [join(): pl.pallas_call(functools.partial(join_kernel, (count, slices)), out_shape...]
where the time goes in v5:
time: 49.3 us; the launch traced here: 49 us
  Pallas kernels  47.9 us (97%)
  other arithmetic  0.84 us (2%)
    pallas_call x1, Pallas kernels, join(): pl.pallas_call(functools.partial(join_kernel, (count, slices)), out_shape...  47.9 us

profile of v5, /device:TPU:0, one launch (start us, length us, event | category | flops | bytes accessed | tf_op | source)
XLA Modules:
  0.0 49.0 jit_solution(9240994760195975377)
XLA Ops:
  0.0 0.1 halo_exchange.1
  0.1 0.2 conditional.1
  0.3 47.9 %join_agents.1 = f32[256,512]{1,0:T(8,128)S(1)} custom-call(s32[1,256]{1,0:T(1,128)} %bitcast.31, s32[1,256]{1,0:T(1,128)} %bitcast.32, s32[1,256]{1,0:T(1,128)} %bitcast.33, f32[128,128]{1,0:T(8,128)} %bitcast.30, f32[256,512]{1,0:T(8,128)S(1)} %get-tuple-element.55.reflect_ref, f32[256,512]{1,0:T(8,128)} %bitcast.24, bf16[256,128,128]{2,1,0:T(8,128)(2,1)} %blocks_hbm.1), custom_call_target="tpu_custom_call" | custom-call | tf_op jit(solution)/shard_map/join_agents/pallas_call | solution.py:800
  48.2 0.8 %broadcast_multiply_fusion = f32[256,512]{1,0:T(8,128)} fusion(f32[256,512]{1,0:T(8,128)S(1)} %join_agents.1), kind=kLoop, calls=%fused_computation.10 | loop fusion | flops 131072 | bytes 1048576 | tf_op jit(solution)/shard_map/mul | solution.py:876
  (1 shorter events, 0.0 us)

commit v6 on v5

--- a/solution.py
+++ b/solution.py
@@ -675,6 +675,71 @@
             rest_copy(step, d).wait_send()
         return full[step].reshape(ray_total, slices * LANES)
 
+    middle = chunks // 2
+
+    def half_of(side):
+        return range(side * middle, chunks if side else middle)
+
+    def last_update(side):
+        first, count_here = side * (slices // 2), slices // 2 if side == 0 else slices - slices // 2
+        at = slice(first * LANES, (first + count_here) * LANES)
+        moved = x[:, at] - 0.8 * scatter_rows(tile_hot[...], y[:, at])
+        for z in range(count_here):
+            for t in range(detectors):
+                place = (slice((first + z) * local, (first + z + 1) * local), slice(t * LANES, (t + 1) * LANES))
+                piece = moved[t * local:(t + 1) * local, z * LANES:(z + 1) * LANES]
+                out_ref[place] = 2.0 * piece - cur[place]
+
+    def finish(k, base, others):
+        out_ref[rows_of(k), :] = 2.0 * cur[rows_of(k), :] - base[rows_of(k), :] + others
+
+    def low_part(side, base):
+        mine, rest = half_of(side), half_of(1 - side)
+        for part_of in (rest, mine):
+            if side == 0:
+                last_update(0 if part_of is mine else 1)
+                for k in part_of:
+                    own[k] = out_ref[rows_of(k), :].astype(BF)
+                if part_of is rest:
+                    pl.semaphore_wait(ready.at[0], 2)
+            for k in part_of:
+                to_beside(k).start()
+        for k in mine:
+            to_beside(k).wait_recv()
+            pair[k] = (own[k].astype(F32) + beside[k].astype(F32)).astype(BF)
+            to_across(pair, k).start()
+        for part_of in (mine, rest):
+            for k in part_of:
+                if part_of is rest:
+                    to_beside(k).wait_recv()
+                to_across(pair, k).wait_recv()
+                finish(k, base, beside[k].astype(F32) + across[k].astype(F32))
+        for k in range(chunks):
+            to_beside(k).wait_send()
+        for k in mine:
+            to_across(pair, k).wait_send()
+
+    def high_part(side):
+        mine, rest = half_of(side), half_of(1 - side)
+        for k in range(chunks):
+            to_beside(k).start()
+        for k in range(chunks):
+            to_beside(k).wait_recv()
+            pair[k] = (own[k].astype(F32) + beside[k].astype(F32)).astype(BF)
+            to_across(pair, k).start()
+        for k in mine:
+            to_across(pair, k).wait_recv()
+            to_onward(k).start()
+            finish(k, reflect_ref, beside[k].astype(F32) + across[k].astype(F32))
+        for k in rest:
+            to_onward(k).wait_recv()
+            finish(k, reflect_ref, beside[k].astype(F32) + onward[k].astype(F32))
+        for k in range(chunks):
+            to_beside(k).wait_send()
+            to_across(pair, k).wait_send()
+        for k in mine:
+            to_onward(k).wait_send()
+
     @pl.when(agent == 0)
     def _():
         barrier = pltpu.get_barrier_semaphore()
@@ -710,17 +775,10 @@
                 pl.semaphore_wait(barrier, count - 1)
             picked[...] = gather_rows(ray_turned[...], exchange(step))
             block_sweep(blocks_hbm, held, sems, picked, y, slices, False, False)
-            x[...] = x[...] - 0.8 * scatter_rows(tile_hot[...], y[...])
-
-        for z in range(slices):
-            for t in range(detectors):
-                moved = x[t * local:(t + 1) * local, z * LANES:(z + 1) * LANES]
-                at = (slice(z * local, (z + 1) * local), slice(t * LANES, (t + 1) * LANES))
-                out_ref[at] = 2.0 * moved - cur[at]
-        for k in range(chunks):
-            own[k] = out_ref[rows_of(k), :].astype(BF)
-        out_ref[...] = 2.0 * cur[...] - out_ref[...]
-        pl.semaphore_wait(ready.at[0], 2)
+            if step < DATA_STEPS - 1:
+                x[...] = x[...] - 0.8 * scatter_rows(tile_hot[...], y[...])
+
+        low_part(0, out_ref)
 
     @pl.when(agent != 0)
     def _():
@@ -737,48 +795,23 @@
         for k in range(chunks):
             own[k] = reflect_ref[rows_of(k), :].astype(BF)
         state.wait()
-        out_ref[...] = 2.0 * cur[...] - reflect_ref[...]
         pl.semaphore_wait(barrier, 2)
 
         @pl.when(agent != 3)
         def _():
             pl.semaphore_signal(ready.at[0], inc=1, device_id=(0, me), device_id_type=MESH)
 
-    def add(k, others):
-        out_ref[rows_of(k), :] = out_ref[rows_of(k), :] + others
-
-    @pl.when(agent < 2)
-    def _():
-        for k in range(chunks):
-            to_across(own, k).start()
-            to_beside(k).start()
-        for k in range(chunks):
-            to_beside(k).wait_recv()
-            to_across(own, k).wait_recv()
-            add(k, beside[k].astype(F32) + across[k].astype(F32))
-        for k in range(chunks):
-            to_across(own, k).wait_send()
-            to_beside(k).wait_send()
-
-    @pl.when(agent >= 2)
-    def _():
-        for k in range(chunks):
-            to_beside(k).start()
-        for k in range(chunks):
-            to_beside(k).wait_recv()
-            pair[k] = (own[k].astype(F32) + beside[k].astype(F32)).astype(BF)
-            to_across(pair, k).start()
-        for k in range(chunks):
-            to_across(pair, k).wait_recv()
-            to_onward(k).start()
-            add(k, beside[k].astype(F32) + across[k].astype(F32))
-        for k in range(chunks):
-            to_onward(k).wait_recv()
-            add(k, onward[k].astype(F32))
-        for k in range(chunks):
-            to_beside(k).wait_send()
-            to_across(pair, k).wait_send()
-            to_onward(k).wait_send()
+        @pl.when(agent == 1)
+        def _():
+            low_part(1, reflect_ref)
+
+        @pl.when(agent == 2)
+        def _():
+            high_part(0)
+
+        @pl.when(agent == 3)
+        def _():
+            high_part(1)
 
 
 def idle_kernel(out_ref):
@@ -793,7 +826,7 @@
     blocks_here = blocks.shape[0]
     width = slices * LANES
     rows = slices * local
-    chunks = max(1, rows // 32)
+    chunks = max(2, rows // 32)
     chunk = (chunks, rows // chunks, columns)
     vmem = pl.BlockSpec(memory_space=pltpu.VMEM)
     anywhere = pl.BlockSpec(memory_space=pl.ANY)

time: 49.3 us -> 49.3 us (level)
  no operation moved by 1% of the time
where the time goes in v6:
time: 49.3 us; the launch traced here: 49 us
  Pallas kernels  47.9 us (97%)
  other arithmetic  0.84 us (2%)
    pallas_call x1, Pallas kernels, join(): pl.pallas_call(functools.partial(join_kernel, (count, slices)), out_shape...  47.9 us

profile of v6, /device:TPU:0, one launch (start us, length us, event | category | flops | bytes accessed | tf_op | source)
XLA Modules:
  0.0 49.0 jit_solution(18264090687745629484)
XLA Ops:
  0.0 0.1 halo_exchange.1
  0.1 0.2 conditional.1
  0.3 47.9 %join_agents.1 = f32[256,512]{1,0:T(8,128)S(1)} custom-call(s32[1,256]{1,0:T(1,128)} %bitcast.31, s32[1,256]{1,0:T(1,128)} %bitcast.32, s32[1,256]{1,0:T(1,128)} %bitcast.33, f32[128,128]{1,0:T(8,128)} %bitcast.30, f32[256,512]{1,0:T(8,128)S(1)} %get-tuple-element.55.reflect_ref, f32[256,512]{1,0:T(8,128)} %bitcast.24, bf16[256,128,128]{2,1,0:T(8,128)(2,1)} %blocks_hbm.1), custom_call_target="tpu_custom_call" | custom-call | tf_op jit(solution)/shard_map/join_agents/pallas_call | solution.py:833
  48.1 0.8 %broadcast_multiply_fusion = f32[256,512]{1,0:T(8,128)} fusion(f32[256,512]{1,0:T(8,128)S(1)} %join_agents.1), kind=kLoop, calls=%fused_computation.10 | loop fusion | flops 131072 | bytes 1048576 | tf_op jit(solution)/shard_map/mul | solution.py:909
  (1 shorter events, 0.0 us)

commit v7 on v6

--- a/solution.py
+++ b/solution.py
@@ -12,7 +12,7 @@
 LANES = 128
 STRIPS = 16
 CHUNK = 64
-SPAN = 256
+DEPTH = 2
 BF = jnp.bfloat16
 F32 = jnp.float32
 NATURAL = (0, 1, 2, 3)
@@ -166,8 +166,11 @@
         before = main[side, 2 * pair].astype(F32)
         for t in range(count):
             row = 2 * (pair + t)
-            outside = (at_start & (row < halo)) | (at_end & (row >= rows - halo))
-            v = jnp.maximum(y(t), 0.0) * jnp.where(outside, 0.0, 1.0)
+            v = jnp.maximum(y(t), 0.0)
+            if row < halo:
+                v = v * jnp.where(at_start, 0.0, 1.0)
+            elif row >= rows - halo:
+                v = v * jnp.where(at_end, 0.0, 1.0)
             even_row = v[:, :LANES].reshape(slices, per, STRIPS, LANES)
             odd_row = v[:, LANES:].reshape(slices, per, STRIPS, LANES)
             main[side, row + 1] = even_row.astype(BF)
@@ -175,17 +178,17 @@
             put_edge(side, pair + t, before, even_row)
             before = odd_row
 
-    def first_step(c, carry):
+    def first_step(c):
         parts = []
         for z in range(slices):
-            at = pl.ds(pl.multiple_of(z * stored + 8 * c, 8), 16)
+            at = pl.ds(z * stored + 8 * c, 16)
             parts.append(jnp.concatenate([xs[at, k * groups:(k + 1) * groups] for k in range(6)], axis=0).astype(BF))
         x = jnp.concatenate(parts, axis=1)
         y = lax.dot_general(x, w1[...], (((0,), (0,)), ((), ())), preferred_element_type=F32)
         put_pairs(0, 4 * c, 4, lambda t: y[:, t * 2 * LANES:(t + 1) * 2 * LANES])
-        return carry
-
-    lax.fori_loop(0, rows // 8, first_step, 0)
+
+    for c in range(rows // 8):
+        first_step(c)
 
     def window(side, pair, out_rows):
         parts = [main[side, 2 * pair + a].reshape(span, LANES) for a in range(out_rows + 2)]
@@ -193,31 +196,30 @@
         return jnp.concatenate(parts, axis=1)
 
     pairs = rows // 2 - 2
-    for layer in range(layers):
+    def layer_step(layer, carry):
         source, target = layer % 2, (layer + 1) % 2
-
-        def hidden_step(c, carry):
+        for c in range(pairs // chunk):
             pair = 1 + c * chunk
             x = jnp.concatenate([window(source, pair + t, 2) for t in range(chunk)], axis=0)
             y = jnp.dot(x, wh[layer], preferred_element_type=F32)
             put_pairs(target, pair, chunk, lambda t: y[t * span:(t + 1) * span])
-            return carry
-
-        lax.fori_loop(0, pairs // chunk, hidden_step, 0)
         end = rows // 2 - 1
         put_edge(target, end, main[target, 2 * end].astype(F32), jnp.zeros((slices, per, STRIPS, LANES), F32))
+        return carry
+
+    lax.fori_loop(0, layers, layer_step, 0)
 
     eighths = local // 8
     quad = (lane_iota(span) // 8) % 4
 
-    def last_step(q, carry):
+    def last_step(q):
         x = window(layers % 2, halo // 2 + 4 * q, 8)
         y = jnp.dot(x, wl[...], preferred_element_type=F32)
         gathered_out[q // 4] = jnp.where(quad == q % 4, y, gathered_out[q // 4])
-        return carry
 
     gathered_out[...] = jnp.zeros_like(gathered_out)
-    lax.fori_loop(0, eighths, last_step, 0)
+    for q in range(eighths):
+        last_step(q)
 
     for big in range(gathered_out.shape[0]):
         height = min(32, local - 32 * big)
@@ -541,14 +543,22 @@
 
 def block_step(held, picked, y, slices, transposed, u):
     row = lax.broadcasted_iota(jnp.int32, (8, LANES), 0)
+    upper, even = row < 4, row % 2 == 0
     at = pl.ds(pl.multiple_of(8 * u, 8), 8)
-    p = [picked[at, z * LANES:(z + 1) * LANES] for z in range(slices)]
-    halves = []
+
+    def turned(v):
+        return pltpu.roll(v, 4, 0)
+
+    rows = [[], []]
+    for z in range(0, slices, 2):
+        v, w = (picked[at, (z + i) * LANES:(z + i + 1) * LANES] for i in range(2))
+        rows[0].append(jnp.where(upper, v, turned(w)))
+        rows[1].append(jnp.where(upper, turned(v), w))
+    outs = []
     for t in range(2):
-        sides = []
-        for side in range(2):
-            mask = row // 2 == 2 * t + side
-            sides.append(jnp.concatenate([jnp.where(mask, v, 0.0) for v in p], axis=0))
+        sides = [
+            jnp.concatenate([jnp.where(row % 4 // 2 == side, v, 0.0) for v in rows[t]], axis=0) for side in range(2)
+        ]
         lhs = jnp.concatenate(sides, axis=1).astype(BF)
         m = [held[8 * u + 4 * t + j] for j in range(4)]
         if transposed:
@@ -558,25 +568,23 @@
             top, bottom = jnp.concatenate([m[0], m[1]], axis=1), jnp.concatenate([m[2], m[3]], axis=1)
             dims = (((1,), (0,)), ((), ()))
         rhs = jnp.concatenate([top, bottom], axis=0)
-        halves.append(lax.dot_general(lhs, rhs, dims, preferred_element_type=F32))
-    for z in range(slices):
-        a, b = (h[8 * z:8 * z + 8] for h in halves)
-        low = jnp.where(row < 4, a[:, :LANES], b[:, :LANES])
-        high = jnp.where(row < 4, a[:, LANES:], b[:, LANES:])
-        y[at, z * LANES:(z + 1) * LANES] = jnp.where(row % 2 == 0, low, high)
+        out = lax.dot_general(lhs, rhs, dims, preferred_element_type=F32)
+        outs.append(jnp.where(jnp.concatenate([even] * (slices // 2), axis=0), out[:, :LANES], out[:, LANES:]))
+    for z in range(0, slices, 2):
+        v, w = (o[4 * z:4 * z + 8] for o in outs)
+        y[at, z * LANES:(z + 1) * LANES] = jnp.where(upper, v, turned(w))
+        y[at, (z + 1) * LANES:(z + 2) * LANES] = jnp.where(upper, turned(v), w)
 
 
 def block_sweep(blocks_hbm, held, sems, picked, y, slices, transposed, waiting):
-    span = min(SPAN, held.shape[0])
-
-    def chunk(i, carry):
-        for j in range(span // 8):
-            if waiting and j % (CHUNK // 8) == 0:
-                block_copy(blocks_hbm, held, sems, i * (span // CHUNK) + j // (CHUNK // 8)).wait()
-            block_step(held, picked, y, slices, transposed, i * (span // 8) + j)
-        return carry
-
-    lax.fori_loop(0, held.shape[0] // span, chunk, 0)
+    pieces = held.shape[0] // CHUNK
+    for i in range(pieces):
+        if waiting:
+            block_copy(blocks_hbm, held, sems, i).wait()
+            if i + DEPTH < pieces:
+                block_copy(blocks_hbm, held, sems, i + DEPTH).start()
+        for j in range(CHUNK // 8):
+            block_step(held, picked, y, slices, transposed, i * (CHUNK // 8) + j)
 
 
 def gather_rows(hot, source):
@@ -604,7 +612,7 @@
     chunks, height, columns = own.shape
     local = chunks * height // slices
     detectors = columns // LANES
-    rays_here = fresh.shape[1]
+    rays_here = fresh.shape[2]
     ray_total = count * rays_here
     tiles_here = detectors * local
     blocks_here = held.shape[0]
@@ -633,47 +641,63 @@
     def rows_of(k):
         return slice(k * height, (k + 1) * height)
 
-    def part_copy(step, d):
+    width = slices // 2 * LANES
+
+    def columns_of(h):
+        return slice(h * width, (h + 1) * width)
+
+    def part_copy(step, h, d):
         return pltpu.make_async_remote_copy(
-            src_ref=part.at[step, swap_bits(me, d)],
-            dst_ref=got.at[step, d],
-            send_sem=send1.at[step, d],
-            recv_sem=recv1.at[step, d],
+            src_ref=part.at[step, h, swap_bits(me, d)],
+            dst_ref=got.at[step, h, d],
+            send_sem=send1.at[step, h, d],
+            recv_sem=recv1.at[step, h, d],
             device_id=(agent, swap_bits(me, d)),
             device_id_type=MESH,
         )
 
-    def rest_copy(step, d):
+    def rest_copy(step, h, d):
         return pltpu.make_async_remote_copy(
-            src_ref=fresh.at[step],
-            dst_ref=full.at[step, me],
-            send_sem=send2.at[step, d],
-            recv_sem=recv2.at[step, d],
+            src_ref=fresh.at[step, h],
+            dst_ref=full.at[step, h, me],
+            send_sem=send2.at[step, h, d],
+            recv_sem=recv2.at[step, h, d],
             device_id=(agent, swap_bits(me, d)),
             device_id_type=MESH,
         )
 
-    def exchange(step):
-        for slot in range(count):
-            part[step, slot] = total[slot * rays_here:(slot + 1) * rays_here, :].astype(BF)
-        for d in order:
-            part_copy(step, d).start()
-        own = total[pl.ds(pl.multiple_of(me * rays_here, 8), rays_here), :]
-        measured = [sino_ref[pl.ds(z, rays_here, stride=slices), :] for z in range(slices)]
-        value = own - jnp.concatenate(measured, axis=1)
-        for d in reversed(order):
-            part_copy(step, d).wait_recv()
-            value = value + got[step, d].astype(F32)
-        fresh[step] = value.astype(BF)
-        for d in order:
-            rest_copy(step, d).start()
-        full[step, me] = fresh[step]
-        for d in order:
-            rest_copy(step, d).wait_recv()
-        for d in order:
-            part_copy(step, d).wait_send()
-            rest_copy(step, d).wait_send()
-        return full[step].reshape(ray_total, slices * LANES)
+    def exchange(step, barrier):
+        for h in range(2):
+            total[h] = scatter_rows(ray_hot[...], y[:, columns_of(h)])
+            for slot in range(count):
+                part[step, h, slot] = total[h, slot * rays_here:(slot + 1) * rays_here, :].astype(BF)
+            if step == 0 and h == 0:
+                pl.semaphore_wait(barrier, count - 1)
+            for d in order:
+                part_copy(step, h, d).start()
+        for h in range(2):
+            value = total[h, pl.ds(pl.multiple_of(me * rays_here, 8), rays_here), :]
+            measured = [
+                sino_ref[pl.ds(h * (slices // 2) + z, rays_here, stride=slices), :] for z in range(slices // 2)
+            ]
+            value = value - jnp.concatenate(measured, axis=1)
+            for d in reversed(order):
+                part_copy(step, h, d).wait_recv()
+                value = value + got[step, h, d].astype(F32)
+            fresh[step, h] = value.astype(BF)
+            for d in order:
+                rest_copy(step, h, d).start()
+            full[step, h, me] = fresh[step, h]
+        for h in range(2):
+            for d in order:
+                rest_copy(step, h, d).wait_recv()
+            picked[:, columns_of(h)] = gather_rows(ray_turned[...], full[step, h].reshape(ray_total, width))
+
+    def exchanged(step):
+        for h in range(2):
+            for d in order:
+                part_copy(step, h, d).wait_send()
+                rest_copy(step, h, d).wait_send()
 
     middle = chunks // 2
 
@@ -747,7 +771,7 @@
             pl.semaphore_signal(barrier, inc=1, device_id=(agent, swap_bits(me, d)), device_id_type=MESH)
         for peer in (neighbour, opposite):
             pl.semaphore_signal(barrier, inc=1, device_id=(peer, me), device_id_type=MESH)
-        for i in range(blocks_here // CHUNK):
+        for i in range(min(DEPTH, blocks_here // CHUNK)):
             block_copy(blocks_hbm, held, sems, i).start()
 
         hot_rows = lax.broadcasted_iota(jnp.int32, (ray_total, blocks_here), 0)
@@ -770,11 +794,9 @@
         for step in range(DATA_STEPS):
             picked[...] = gather_rows(tile_turned[...], x[...].astype(BF))
             block_sweep(blocks_hbm, held, sems, picked, y, slices, True, step == 0)
-            total[...] = scatter_rows(ray_hot[...], y[...])
-            if step == 0:
-                pl.semaphore_wait(barrier, count - 1)
-            picked[...] = gather_rows(ray_turned[...], exchange(step))
+            exchange(step, barrier)
             block_sweep(blocks_hbm, held, sems, picked, y, slices, False, False)
+            exchanged(step)
             if step < DATA_STEPS - 1:
                 x[...] = x[...] - 0.8 * scatter_rows(tile_hot[...], y[...])
 
@@ -845,15 +867,15 @@
             pltpu.VMEM((tiles_here, width), F32),
             pltpu.VMEM((blocks_here, width), F32),
             pltpu.VMEM((blocks_here, width), F32),
-            pltpu.VMEM((ray_total, width), F32),
-            pltpu.VMEM((DATA_STEPS, count, rays_here, width), BF),
-            pltpu.VMEM((DATA_STEPS, count, rays_here, width), BF),
-            pltpu.VMEM((DATA_STEPS, rays_here, width), BF),
-            pltpu.VMEM((DATA_STEPS, count, rays_here, width), BF),
+            pltpu.VMEM((2, ray_total, width // 2), F32),
+            pltpu.VMEM((DATA_STEPS, 2, count, rays_here, width // 2), BF),
+            pltpu.VMEM((DATA_STEPS, 2, count, rays_here, width // 2), BF),
+            pltpu.VMEM((DATA_STEPS, 2, rays_here, width // 2), BF),
+            pltpu.VMEM((DATA_STEPS, 2, count, rays_here, width // 2), BF),
         ]
         + [pltpu.VMEM(chunk, BF)] * 5
         + [pltpu.SemaphoreType.DMA((1,)), pltpu.SemaphoreType.DMA((blocks_here // CHUNK,))]
-        + [pltpu.SemaphoreType.DMA((DATA_STEPS, count))] * 4
+        + [pltpu.SemaphoreType.DMA((DATA_STEPS, 2, count))] * 4
         + [pltpu.SemaphoreType.REGULAR((1,))]
         + [pltpu.SemaphoreType.DMA((chunks,))] * 6,
         compiler_params=pltpu.CompilerParams(

time: 49.3 us -> 57 us (1.16)
  Pallas kernels: 47.9 us -> 55.6 us
    pallas_call x1, Pallas kernels: 47.9 us -> 55.5 us  [join(): pl.pallas_call(functools.partial(join_kernel, (count, slices)), out_shape...]
where the time goes in v7:
time: 57 us; the launch traced here: 56.7 us
  Pallas kernels  55.6 us (98%)
  other arithmetic  0.84 us (1%)
    pallas_call x1, Pallas kernels, join(): pl.pallas_call(functools.partial(join_kernel, (count, slices)), out_shape...  55.5 us

profile of v7, /device:TPU:0, one launch (start us, length us, event | category | flops | bytes accessed | tf_op | source)
XLA Modules:
  0.0 56.7 jit_solution(4412046901462385345)
XLA Ops:
  0.0 0.1 halo_exchange.1
  0.1 0.3 conditional.1
  0.3 55.5 %join_agents.1 = f32[256,512]{1,0:T(8,128)S(1)} custom-call(s32[1,256]{1,0:T(1,128)} %bitcast.31, s32[1,256]{1,0:T(1,128)} %bitcast.32, s32[1,256]{1,0:T(1,128)} %bitcast.33, f32[128,128]{1,0:T(8,128)} %bitcast.30, f32[256,512]{1,0:T(8,128)S(1)} %get-tuple-element.55.reflect_ref, f32[256,512]{1,0:T(8,128)} %bitcast.24, bf16[256,128,128]{2,1,0:T(8,128)(2,1)} %blocks_hbm.1), custom_call_target="tpu_custom_call" | custom-call | tf_op jit(solution)/shard_map/join_agents/pallas_call | solution.py:855
  55.9 0.8 %broadcast_multiply_fusion = f32[256,512]{1,0:T(8,128)} fusion(f32[256,512]{1,0:T(8,128)S(1)} %join_agents.1), kind=kLoop, calls=%fused_computation.10 | loop fusion | flops 131072 | bytes 1048576 | tf_op jit(solution)/shard_map/mul | solution.py:931
  (1 shorter events, 0.0 us)

commit v8 on v7

--- a/solution.py
+++ b/solution.py
@@ -106,7 +106,7 @@
 
 
 def axial_kernel(plan, edges_ref, cur_ref, cf_ref, ch_ref, cl_ref, out_ref, main, edge, w1, wh, wl, raw, xs, place, back, gathered_out):
-    halo, chunk = plan
+    halo = plan
     slices, local, columns = cur_ref.shape
     rows = local + 2 * halo
     stored = rows + 8
@@ -167,7 +167,10 @@
         for t in range(count):
             row = 2 * (pair + t)
             v = jnp.maximum(y(t), 0.0)
-            if row < halo:
+            if not isinstance(row, int):
+                outside = (at_start & (row < halo)) | (at_end & (row >= rows - halo))
+                v = v * jnp.where(outside, 0.0, 1.0)
+            elif row < halo:
                 v = v * jnp.where(at_start, 0.0, 1.0)
             elif row >= rows - halo:
                 v = v * jnp.where(at_end, 0.0, 1.0)
@@ -196,30 +199,36 @@
         return jnp.concatenate(parts, axis=1)
 
     pairs = rows // 2 - 2
-    def layer_step(layer, carry):
+    run = max(n for n in range(1, 18) if pairs % n == 0)
+    for layer in range(layers):
         source, target = layer % 2, (layer + 1) % 2
-        for c in range(pairs // chunk):
-            pair = 1 + c * chunk
-            x = jnp.concatenate([window(source, pair + t, 2) for t in range(chunk)], axis=0)
-            y = jnp.dot(x, wh[layer], preferred_element_type=F32)
-            put_pairs(target, pair, chunk, lambda t: y[t * span:(t + 1) * span])
+
+        def hidden_steps(c, carry):
+            for j in range(run):
+                pair = 1 + c * run + j
+                y = jnp.dot(window(source, pair, 2), wh[layer], preferred_element_type=F32)
+                put_pairs(target, pair, 1, lambda t: y)
+            return carry
+
+        lax.fori_loop(0, pairs // run, hidden_steps, 0)
         end = rows // 2 - 1
         put_edge(target, end, main[target, 2 * end].astype(F32), jnp.zeros((slices, per, STRIPS, LANES), F32))
-        return carry
-
-    lax.fori_loop(0, layers, layer_step, 0)
 
     eighths = local // 8
     quad = (lane_iota(span) // 8) % 4
 
-    def last_step(q):
-        x = window(layers % 2, halo // 2 + 4 * q, 8)
-        y = jnp.dot(x, wl[...], preferred_element_type=F32)
-        gathered_out[q // 4] = jnp.where(quad == q % 4, y, gathered_out[q // 4])
-
-    gathered_out[...] = jnp.zeros_like(gathered_out)
-    for q in range(eighths):
-        last_step(q)
+    four = 4 if eighths % 4 == 0 else eighths
+
+    def last_steps(c, carry):
+        value = jnp.zeros((span, LANES), F32)
+        for j in range(four):
+            x = window(layers % 2, halo // 2 + 4 * (c * four + j), 8)
+            y = jnp.dot(x, wl[...], preferred_element_type=F32)
+            value = jnp.where(quad == j, y, value)
+        gathered_out[c] = value
+        return carry
+
+    lax.fori_loop(0, eighths // four, last_steps, 0)
 
     for big in range(gathered_out.shape[0]):
         height = min(32, local - 32 * big)
@@ -241,7 +250,7 @@
     stored = rows + 8
     whole = pl.BlockSpec(memory_space=pltpu.VMEM)
     return pl.pallas_call(
-        functools.partial(axial_kernel, (halo, 2)),
+        functools.partial(axial_kernel, halo),
         out_shape=jax.ShapeDtypeStruct(current.shape, F32),
         in_specs=[whole] * 5,
         out_specs=whole,

time: 57 us -> 43.7 us (0.77)
  Pallas kernels: 55.6 us -> 42 us
    pallas_call x1, Pallas kernels: 55.5 us -> 41.9 us  [join(): pl.pallas_call(functools.partial(join_kernel, (count, slices)), out_shape...]
where the time goes in v8:
time: 43.7 us; the launch traced here: 43.1 us
  Pallas kernels  42 us (96%)
  other arithmetic  0.84 us (2%)
    pallas_call x1, Pallas kernels, join(): pl.pallas_call(functools.partial(join_kernel, (count, slices)), out_shape...  41.9 us

profile of v8, /device:TPU:0, one launch (start us, length us, event | category | flops | bytes accessed | tf_op | source)
XLA Modules:
  0.0 43.1 jit_solution(12847234282130537202)
XLA Ops:
  0.0 0.1 halo_exchange.1
  0.1 0.2 conditional.1
  0.3 41.9 %join_agents.1 = f32[256,512]{1,0:T(8,128)S(1)} custom-call(s32[1,256]{1,0:T(1,128)} %bitcast.31, s32[1,256]{1,0:T(1,128)} %bitcast.32, s32[1,256]{1,0:T(1,128)} %bitcast.33, f32[128,128]{1,0:T(8,128)} %bitcast.30, f32[256,512]{1,0:T(8,128)S(1)} %get-tuple-element.55.reflect_ref, f32[256,512]{1,0:T(8,128)} %bitcast.24, bf16[256,128,128]{2,1,0:T(8,128)(2,1)} %blocks_hbm.1), custom_call_target="tpu_custom_call" | custom-call | tf_op jit(solution)/shard_map/join_agents/pallas_call | solution.py:864
  42.2 0.8 %broadcast_multiply_fusion = f32[256,512]{1,0:T(8,128)} fusion(f32[256,512]{1,0:T(8,128)S(1)} %join_agents.1), kind=kLoop, calls=%fused_computation.10 | loop fusion | flops 131072 | bytes 1048576 | tf_op jit(solution)/shard_map/mul | solution.py:940
  (1 shorter events, 0.0 us)

commit v9 on v8

--- a/solution.py
+++ b/solution.py
@@ -11,7 +11,7 @@
 MESH = pl.DeviceIdType.MESH
 LANES = 128
 STRIPS = 16
-CHUNK = 64
+CHUNK = 96
 DEPTH = 2
 BF = jnp.bfloat16
 F32 = jnp.float32
@@ -546,7 +546,7 @@
 
 
 def block_copy(blocks_hbm, held, sems, i):
-    at = pl.ds(i * CHUNK, CHUNK)
+    at = pl.ds(i * CHUNK, min(CHUNK, held.shape[0] - i * CHUNK))
     return pltpu.make_async_copy(blocks_hbm.at[at], held.at[at], sems.at[i])
 
 
@@ -586,14 +586,14 @@
 
 
 def block_sweep(blocks_hbm, held, sems, picked, y, slices, transposed, waiting):
-    pieces = held.shape[0] // CHUNK
+    pieces = pl.cdiv(held.shape[0], CHUNK)
     for i in range(pieces):
         if waiting:
             block_copy(blocks_hbm, held, sems, i).wait()
             if i + DEPTH < pieces:
                 block_copy(blocks_hbm, held, sems, i + DEPTH).start()
-        for j in range(CHUNK // 8):
-            block_step(held, picked, y, slices, transposed, i * (CHUNK // 8) + j)
+        for u in range(i * CHUNK // 8, min((i + 1) * CHUNK, held.shape[0]) // 8):
+            block_step(held, picked, y, slices, transposed, u)
 
 
 def gather_rows(hot, source):
@@ -724,7 +724,7 @@
                 out_ref[place] = 2.0 * piece - cur[place]
 
     def finish(k, base, others):
-        out_ref[rows_of(k), :] = 2.0 * cur[rows_of(k), :] - base[rows_of(k), :] + others
+        out_ref[rows_of(k), :] = 0.5 * cur[rows_of(k), :] + 0.25 * (others - base[rows_of(k), :])
 
     def low_part(side, base):
         mine, rest = half_of(side), half_of(1 - side)
@@ -780,7 +780,7 @@
             pl.semaphore_signal(barrier, inc=1, device_id=(agent, swap_bits(me, d)), device_id_type=MESH)
         for peer in (neighbour, opposite):
             pl.semaphore_signal(barrier, inc=1, device_id=(peer, me), device_id_type=MESH)
-        for i in range(min(DEPTH, blocks_here // CHUNK)):
+        for i in range(min(DEPTH, pl.cdiv(blocks_here, CHUNK))):
             block_copy(blocks_hbm, held, sems, i).start()
 
         hot_rows = lax.broadcasted_iota(jnp.int32, (ray_total, blocks_here), 0)
@@ -883,7 +883,7 @@
             pltpu.VMEM((DATA_STEPS, 2, count, rays_here, width // 2), BF),
         ]
         + [pltpu.VMEM(chunk, BF)] * 5
-        + [pltpu.SemaphoreType.DMA((1,)), pltpu.SemaphoreType.DMA((blocks_here // CHUNK,))]
+        + [pltpu.SemaphoreType.DMA((1,)), pltpu.SemaphoreType.DMA((pl.cdiv(blocks_here, CHUNK),))]
         + [pltpu.SemaphoreType.DMA((DATA_STEPS, 2, count))] * 4
         + [pltpu.SemaphoreType.REGULAR((1,))]
         + [pltpu.SemaphoreType.DMA((chunks,))] * 6,
@@ -937,7 +937,7 @@
     joined = join(
         block_angle, block_detector, block_tile, sinogram, reflect, current, blocks, lax.axis_size("tile")
     )
-    return (0.25 * joined)[None]
+    return joined[None]
 
 
 def solution(mesh):

time: 43.7 us -> 43.4 us (level)
  other arithmetic: 0.84 us -> 0 us
  local copies, waits for them, and re-layouts: 0 us -> 0.8 us
    mul x1 -> x0, other arithmetic: 0.84 us -> none  [per_device(): return (0.25 * joined)[None]]
    unnamed x0 -> x1, local copies, waits for them, and re-layouts: none -> 0.8 us
where the time goes in v9:
time: 43.4 us; the launch traced here: 43 us
  Pallas kernels  42 us (97%)
  local copies, waits for them, and re-layouts  0.8 us (2%)
    pallas_call x1, Pallas kernels, join(): pl.pallas_call(functools.partial(join_kernel, (count, slices)), out_shape...  41.9 us

profile of v9, /device:TPU:0, one launch (start us, length us, event | category | flops | bytes accessed | tf_op | source)
XLA Modules:
  0.0 43.0 jit_solution(18202336439090925030)
XLA Ops:
  0.0 0.1 halo_exchange.1
  0.1 0.2 conditional.1
  0.3 41.9 %join_agents.1 = f32[256,512]{1,0:T(8,128)S(1)} custom-call(s32[1,256]{1,0:T(1,128)} %bitcast.32, s32[1,256]{1,0:T(1,128)} %bitcast.33, s32[1,256]{1,0:T(1,128)} %bitcast.34, f32[128,128]{1,0:T(8,128)} %bitcast.31, f32[256,512]{1,0:T(8,128)S(1)} %get-tuple-element.55.reflect_ref, f32[256,512]{1,0:T(8,128)} %bitcast.25, bf16[256,128,128]{2,1,0:T(8,128)(2,1)} %blocks_hbm.1), custom_call_target="tpu_custom_call" | custom-call | tf_op jit(solution)/shard_map/join_agents/pallas_call | solution.py:864
  42.2 0.8 %copy.19 = f32[1,4,64,512]{3,2,1,0:T(8,128)} copy(f32[1,4,64,512]{3,2,1,0:T(8,128)S(1)} %bitcast.21) | data formatting | bytes 1048576
  (1 shorter events, 0.0 us)

commit v10 on v9

--- a/solution.py
+++ b/solution.py
@@ -677,7 +677,7 @@
 
     def exchange(step, barrier):
         for h in range(2):
-            total[h] = scatter_rows(ray_hot[...], y[:, columns_of(h)])
+            total[h] = gather_rows(ray_hot[...], y[:, columns_of(h)].astype(BF))
             for slot in range(count):
                 part[step, h, slot] = total[h, slot * rays_here:(slot + 1) * rays_here, :].astype(BF)
             if step == 0 and h == 0:

time: 43.4 us -> 43.3 us (level)
  no operation moved by 1% of the time
where the time goes in v10:
time: 43.3 us; the launch traced here: 43 us
  Pallas kernels  42 us (97%)
  local copies, waits for them, and re-layouts  0.8 us (2%)
    pallas_call x1, Pallas kernels, join(): pl.pallas_call(functools.partial(join_kernel, (count, slices)), out_shape...  41.9 us

profile of v10, /device:TPU:0, one launch (start us, length us, event | category | flops | bytes accessed | tf_op | source)
XLA Modules:
  0.0 43.0 jit_solution(5137821314299891089)
XLA Ops:
  0.0 0.1 halo_exchange.1
  0.1 0.2 conditional.1
  0.3 41.9 %join_agents.1 = f32[256,512]{1,0:T(8,128)S(1)} custom-call(s32[1,256]{1,0:T(1,128)} %bitcast.32, s32[1,256]{1,0:T(1,128)} %bitcast.33, s32[1,256]{1,0:T(1,128)} %bitcast.34, f32[128,128]{1,0:T(8,128)} %bitcast.31, f32[256,512]{1,0:T(8,128)S(1)} %get-tuple-element.55.reflect_ref, f32[256,512]{1,0:T(8,128)} %bitcast.25, bf16[256,128,128]{2,1,0:T(8,128)(2,1)} %blocks_hbm.1), custom_call_target="tpu_custom_call" | custom-call | tf_op jit(solution)/shard_map/join_agents/pallas_call | solution.py:864
  42.2 0.8 %copy.19 = f32[1,4,64,512]{3,2,1,0:T(8,128)} copy(f32[1,4,64,512]{3,2,1,0:T(8,128)S(1)} %bitcast.21) | data formatting | bytes 1048576
  (1 shorter events, 0.0 us)
